TPU v7x, 8 devices: a whole 2x2x1 slice. The times are simulated.
8 devices in a mesh: dp: 1 (over z), cz: 2 (over y), cy: 2 (over x), cx: 2 (over core).
Axes of the slice: x: 2, y: 2, z: 1, core: 2. Of those that a mesh axis runs over, the one named last changes fastest.
Arguments:
- x_act: bfloat16 [4096, 2560], P(('dp', 'cx', 'cz'), 'cy')
- w_up: bfloat16 [2560, 10240], P('cy', ('cz', 'cx'))
- w_down: bfloat16 [10240, 2560], P('cz', ('cy', 'cx'))
- z_grad: bfloat16 [4096, 2560], P(('dp', 'cx', 'cz'), 'cy')
Outputs:
- output 1: bfloat16 [4096, 2560], P(('dp', 'cx', 'cz'), 'cy')
- output 2: bfloat16 [2560, 10240], P(('dp', 'cy'), ('cz', 'cx'))
- output 3: bfloat16 [10240, 2560], P(('dp', 'cz'), ('cy', 'cx'))
All inputs are finite; a program needn't handle non-finite values.
Results may differ from a plain program's by a relative error of at most 0.0115215.
Values are sent between devices in bfloat16 or wider.
A program may use at most 1 GiB of HBM per device.

v0:
```python
import math
import jax
import jax.numpy as jnp
from jax import lax
from jax.sharding import PartitionSpec as P

GELU_COEF = 0.044715
SQRT_TWO_PI = math.sqrt(2.0 / math.pi)
CONTRACT_LAST = (((1,), (1,)), ((), ()))
CONTRACT_FIRST = (((0,), (0,)), ((), ()))


def gelu_parts(pre_act):
    inner_arg = SQRT_TWO_PI * (pre_act + GELU_COEF * pre_act * pre_act * pre_act)
    tanh_val = jnp.tanh(inner_arg)
    gelu_val = 0.5 * pre_act * (1.0 + tanh_val)
    gelu_slope = 0.5 * (1.0 + tanh_val) + 0.5 * pre_act * (1.0 - tanh_val * tanh_val) * SQRT_TWO_PI * (1.0 + 3.0 * GELU_COEF * pre_act * pre_act)
    return gelu_val, gelu_slope


def solution(mesh):
    row_spec = P(("dp", "cx", "cz"), "cy")
    up_spec = P("cy", ("cz", "cx"))
    down_spec = P("cz", ("cy", "cx"))
    up_out = P(("dp", "cy"), ("cz", "cx"))
    down_out = P(("dp", "cz"), ("cy", "cx"))

    def local_step(x_act, w_up, w_down, z_grad):
        x_full = lax.all_gather(x_act, "cz", axis=0, tiled=True)
        up_full = lax.all_gather(w_up, "cx", axis=1, tiled=True)
        pre_part = jnp.dot(x_full, up_full, preferred_element_type=jnp.float32)
        pre_sum = lax.psum_scatter(pre_part, "cy", scatter_dimension=0, tiled=True)
        pre_act = pre_sum.astype(jnp.bfloat16).astype(jnp.float32)
        gelu_val, gelu_slope = gelu_parts(pre_act)
        hidden = gelu_val.astype(jnp.bfloat16)
        z_full = lax.all_gather(z_grad, "cz", axis=0, tiled=True)
        down_full = lax.all_gather(w_down, "cx", axis=1, tiled=True)
        h_part = lax.dot_general(z_full, down_full, CONTRACT_LAST, preferred_element_type=jnp.float32)
        h_grad = lax.psum_scatter(h_part, "cy", scatter_dimension=0, tiled=True)
        pre_grad = (h_grad * gelu_slope).astype(jnp.bfloat16)
        hidden_full = lax.all_gather(hidden, "cy", axis=0, tiled=True)
        down_part = lax.dot_general(hidden_full, z_full, CONTRACT_FIRST, preferred_element_type=jnp.float32)
        down_grad = lax.psum_scatter(down_part, "cx", scatter_dimension=1, tiled=True).astype(jnp.bfloat16)
        grad_full = lax.all_gather(pre_grad, "cy", axis=0, tiled=True)
        x_part = lax.dot_general(grad_full, up_full, CONTRACT_LAST, preferred_element_type=jnp.float32)
        x_grad = lax.psum_scatter(x_part, "cz", scatter_dimension=0, tiled=True).astype(jnp.bfloat16)
        up_part = lax.dot_general(x_full, grad_full, CONTRACT_FIRST, preferred_element_type=jnp.float32)
        up_grad = lax.psum_scatter(up_part, "cx", scatter_dimension=1, tiled=True).astype(jnp.bfloat16)
        return (x_grad, up_grad, down_grad)

    return jax.shard_map(local_step, mesh=mesh, in_specs=(row_spec, up_spec, down_spec, row_spec), out_specs=(row_spec, up_out, down_out), check_vma=False)
```

profile of v0, /device:TPU:0, one launch (start us, length us, event | category | flops | bytes accessed | tf_op | source)
XLA Modules:
  0.0 1830.6 jit_solution(2434056662827597753)
XLA Ops:
  7.2 0.7 all-gather.7.cloned.1.call-update
  7.9 0.7 all-gather.9.cloned.1.call-update
  8.7 0.7 all-gather.11.cloned.1.call-update
  9.4 0.5 all-gather.13.cloned.1.call-update
  10.0 0.0 reduce-scatter.16.cloned.1.call-start
  10.0 68.5 %all-gather.7.cloned.1.call-done = bf16[2048,1280]{1,0:T(8,128)(2,1)} async-done(((bf16[1024,1280]{1,0:T(8,128)(2,1)}), bf16[2048,1280]{1,0:T(8,128)(2,1)}) %all-gather.7.cloned.1.call-update) | async-done | bytes 5242896 | tf_op jit(solution)/shard_map/all_gather | solution.py:36
  78.5 24.9 %all-gather.9.cloned.1.call-done = bf16[5120,1280]{1,0:T(8,128)(2,1)} async-done(((bf16[5120,640]{1,0:T(8,128)(2,1)}), bf16[5120,1280]{1,0:T(8,128)(2,1)}) %all-gather.9.cloned.1.call-update) | async-done | bytes 13107216 | tf_op jit(solution)/shard_map/all_gather | solution.py:37
  103.5 34.9 %fusion.11 = f32[2048,5120]{1,0:T(8,128)} fusion(bf16[2048,1280]{1,0:T(8,128)(2,1)} %all-gather.7.cloned.1.call-done, bf16[5120,1280]{1,0:T(8,128)(2,1)} %all-gather.9.cloned.1.call-done), kind=kOutput, calls=%fused_computation.19 | convolution fusion | flops 26843545600 | bytes 60293120 | tf_op jit(solution)/shard_map/dot_general | solution.py:38
  138.4 0.0 reduce-scatter.18.cloned.1.call-start
  138.4 34.0 %all-gather.11.cloned.1.call-done = bf16[2048,1280]{1,0:T(8,128)(2,1)} async-done(((bf16[1024,1280]{1,0:T(8,128)(2,1)}), bf16[2048,1280]{1,0:T(8,128)(2,1)}) %all-gather.11.cloned.1.call-update) | async-done | bytes 5242896 | tf_op jit(solution)/shard_map/all_gather | solution.py:29
  172.4 24.8 %all-gather.13.cloned.1.call-done = bf16[1280,5120]{1,0:T(8,128)(2,1)} async-done(((bf16[1280,2560]{1,0:T(8,128)(2,1)}), bf16[1280,5120]{1,0:T(8,128)(2,1)}) %all-gather.13.cloned.1.call-update) | async-done | bytes 13107216 | tf_op jit(solution)/shard_map/all_gather | solution.py:30
  197.2 34.7 %fusion.12 = f32[2048,5120]{1,0:T(8,128)} fusion(bf16[2048,1280]{1,0:T(8,128)(2,1)} %all-gather.11.cloned.1.call-done, bf16[1280,5120]{1,0:T(8,128)(2,1)} %all-gather.13.cloned.1.call-done), kind=kOutput, calls=%fused_computation.20 | convolution fusion | flops 26843545600 | bytes 60293120 | tf_op jit(solution)/shard_map/dot_general | solution.py:31
  231.9 0.2 all-gather.15.cloned.1.call-start
  232.1 424.5 %reduce-scatter.16.cloned.1.call-done = f32[1024,5120]{1,0:T(8,128)} async-done(((f32[2048,5120]{1,0:T(8,128)}), f32[1024,5120]{1,0:T(8,128)}) %reduce-scatter.16.cloned.1.call-update) | async-done | bytes 20971536
  656.6 458.3 %reduce-scatter.18.cloned.1.call-done = f32[1024,5120]{1,0:T(8,128)} async-done(((f32[2048,5120]{1,0:T(8,128)}), f32[1024,5120]{1,0:T(8,128)}) %reduce-scatter.18.cloned.1.call-update) | async-done | bytes 20971536
  1114.9 27.2 %fusion.7 = (bf16[1024,5120]{1,0:T(8,128)(2,1)}, bf16[1024,5120]{1,0:T(8,128)(2,1)}) fusion(f32[1024,5120]{1,0:T(8,128)} %reduce-scatter.18.cloned.1.call-done, f32[1024,5120]{1,0:T(8,128)} %reduce-scatter.16.cloned.1.call-done), kind=kLoop, calls=%fused_computation.15 | loop fusion | flops 120586240 | bytes 62914560 | tf_op jit(solution)/shard_map/convert_element_type | solution.py:35
  1142.1 0.0 all-gather.17.cloned.1.call-start
  1142.2 0.7 all-gather.17.cloned.1.call-update
  1142.9 244.3 %all-gather.15.cloned.1.call-done = bf16[2048,5120]{1,0:T(8,128)(2,1)} async-done(((bf16[1024,5120]{1,0:T(8,128)(2,1)}), bf16[2048,5120]{1,0:T(8,128)(2,1)}) %all-gather.15.cloned.1.call-update) | async-done | bytes 20971536 | tf_op jit(solution)/shard_map/all_gather | solution.py:44
  1387.2 35.8 %fusion.13 = f32[2048,1280]{1,0:T(8,128)} fusion(bf16[2048,5120]{1,0:T(8,128)(2,1)} %all-gather.15.cloned.1.call-done, bf16[1280,5120]{1,0:T(8,128)(2,1)} %all-gather.13.cloned.1.call-done), kind=kOutput, calls=%fused_computation.21 | convolution fusion | flops 26843545600 | bytes 44564480 | tf_op jit(solution)/shard_map/dot_general | solution.py:45
  1423.0 0.3 reduce-scatter.12.cloned.1.call-start
  1423.3 34.8 %convolution_bitcast_fusion = f32[1280,5120]{0,1:T(8,128)} fusion(bf16[2048,5120]{1,0:T(8,128)(2,1)} %all-gather.15.cloned.1.call-done, bf16[2048,1280]{1,0:T(8,128)(2,1)} %all-gather.11.cloned.1.call-done), kind=kOutput, calls=%fused_computation.9 | convolution fusion | flops 26843545600 | bytes 52428800 | tf_op jit(solution)/shard_map/dot_general | solution.py:47
  1458.1 0.3 reduce-scatter.14.cloned.1.call-start
  1458.4 175.3 %all-gather.17.cloned.1.call-done = bf16[2048,5120]{1,0:T(8,128)(2,1)} async-done(((bf16[1024,5120]{1,0:T(8,128)(2,1)}), bf16[2048,5120]{1,0:T(8,128)(2,1)}) %all-gather.17.cloned.1.call-update) | async-done | bytes 20971536 | tf_op jit(solution)/shard_map/all_gather | solution.py:41
  1633.8 34.7 %fusion.14 = f32[5120,1280]{1,0:T(8,128)} fusion(bf16[2048,5120]{1,0:T(8,128)(2,1)} %all-gather.17.cloned.1.call-done, bf16[2048,1280]{1,0:T(8,128)(2,1)} %all-gather.7.cloned.1.call-done), kind=kOutput, calls=%fused_computation.22 | convolution fusion | flops 26843545600 | bytes 52428800 | tf_op jit(solution)/shard_map/dot_general | solution.py:42
  1668.5 86.7 %reduce-scatter.10.cloned.1.call-done = f32[1024,1280]{1,0:T(8,128)} async-done(((f32[2048,1280]{1,0:T(8,128)}), f32[1024,1280]{1,0:T(8,128)}) %reduce-scatter.10.cloned.1.call-update) | async-done | bytes 5242896 | tf_op jit(solution)/shard_map/reduce_scatter | solution.py:46
  1755.1 4.2 convert_element_type.24
  1759.4 25.5 %reduce-scatter.12.cloned.1.call-done = f32[1280,2560]{0,1:T(8,128)} async-done(((f32[1280,5120]{0,1:T(8,128)}), f32[1280,2560]{0,1:T(8,128)}) %reduce-scatter.12.cloned.1.call-update) | async-done | bytes 13107216 | tf_op jit(solution)/shard_map/reduce_scatter | solution.py:48
  1784.9 8.1 convert_element_type.25
  1793.0 9.5 copy.8
  1802.5 13.3 reduce-scatter.14.cloned.1.call-done
  1815.9 8.2 convert_element_type.27
  (11 shorter events, 0.3 us)
Async XLA Ops:
  7.2 71.4 %all-gather.7.cloned.1.call-start = ((), (), s32[]{:S(2)}) async-start(), calls=%async_computation.5 | async-start | bytes 7864320 | tf_op jit(solution)/shard_map/all_gather | solution.py:36
  7.9 95.6 %all-gather.9.cloned.1.call-start = ((), (), s32[]{:S(2)}) async-start(), calls=%async_computation.6 | async-start | bytes 19660800 | tf_op jit(solution)/shard_map/all_gather | solution.py:37
  8.6 163.7 %all-gather.11.cloned.1.call-start = ((), (), s32[]{:S(2)}) async-start(), calls=%async_computation.7 | async-start | bytes 7864320 | tf_op jit(solution)/shard_map/all_gather | solution.py:29
  9.4 187.8 %all-gather.13.cloned.1.call-start = ((), (), s32[]{:S(2)}) async-start(), calls=%async_computation.8 | async-start | bytes 19660800 | tf_op jit(solution)/shard_map/all_gather | solution.py:30
  10.0 646.7 %reduce-scatter.16.cloned.1.call-start = ((), (), s32[]{:S(2)}) async-start(), calls=%async_computation.14 | async-start | bytes 62914560
  138.4 976.5 %reduce-scatter.18.cloned.1.call-start = ((), (), s32[]{:S(2)}) async-start(), calls=%async_computation.15 | async-start | bytes 62914560
  231.9 1155.3 %all-gather.15.cloned.1.call-start = ((), (), s32[]{:S(2)}) async-start(), calls=%async_computation.9 | async-start | bytes 31457280 | tf_op jit(solution)/shard_map/all_gather | solution.py:44
  1142.1 491.7 %all-gather.17.cloned.1.call-start = ((), (), s32[]{:S(2)}) async-start(), calls=%async_computation.12 | async-start | bytes 31457280 | tf_op jit(solution)/shard_map/all_gather | solution.py:41
  1142.9 612.3 %reduce-scatter.10.cloned.1.call-start = ((), (), s32[]{:S(2)}) async-start(), calls=%async_computation.10 | async-start | bytes 15728640 | tf_op jit(solution)/shard_map/reduce_scatter | solution.py:46
  1423.0 361.9 %reduce-scatter.12.cloned.1.call-start = ((), (), s32[]{:S(2)}) async-start(), calls=%async_computation.11 | async-start | bytes 39321600 | tf_op jit(solution)/shard_map/reduce_scatter | solution.py:48
  1458.1 357.7 %reduce-scatter.14.cloned.1.call-start = ((), (), s32[]{:S(2)}) async-start(), calls=%async_computation.13 | async-start | bytes 39321600 | tf_op jit(solution)/shard_map/reduce_scatter | solution.py:43
Sparse Core Ops, SparseCore 0:
  9.5 69.0 all-gather.6
  80.1 23.3 all-gather.8
  105.0 67.3 all-gather.10
  173.8 23.3 all-gather.12
  199.3 457.2 reduce-scatter.15
  658.8 456.1 reduce-scatter.17
  1142.2 244.9 all-gather.14
  1388.8 244.9 all-gather.16
  1636.0 119.0 reduce-scatter.9
  1757.2 27.5 reduce-scatter.11
  1787.1 28.6 reduce-scatter.13
where the time goes:
time: 1830 us
  waiting for transfers between devices  1580 us (86%)
  matrix products  175 us (10%)
  other arithmetic  47.7 us (3%)
    unnamed x13, waiting for transfers between devices  886 us
    all_gather x1, waiting for transfers between devices, local_step(): grad_full = lax.all_gather(pre_grad, 'cy', axis=0, tiled=True)  244 us
    all_gather x1, waiting for transfers between devices, local_step(): hidden_full = lax.all_gather(hidden, 'cy', axis=0, tiled=True)  175 us
    reduce_scatter x1, waiting for transfers between devices, local_step(): lax.psum_scatter(x_part, 'cz', scatter_dimension=0, tiled=True)  86.7 us
    all_gather x1, waiting for transfers between devices, local_step(): z_full = lax.all_gather(z_grad, 'cz', axis=0, tiled=True)  68.5 us
  transfers between devices with their start and end apart: 11, of which 11 were waited for; matrix products, arithmetic and copies ran while one was open for 11% of the time, Pallas kernels for 0%

commit v1 on v0

v1 whole, which is shorter than its diff:
```python
import math
import jax
import jax.numpy as jnp
from jax import lax
from jax.experimental import pallas as pl
from jax.experimental.pallas import tpu as pltpu
from jax.sharding import PartitionSpec as P

GELU_COEF = 0.044715
SQRT_TWO_PI = math.sqrt(2.0 / math.pi)
LAST = (((1,), (1,)), ((), ()))
FIRST = (((0,), (0,)), ((), ()))
F32 = jnp.float32
BF16 = jnp.bfloat16
MESH = pl.DeviceIdType.MESH


W = 256
RB = 512
AHEAD = 3
SLOTS = 3


def gelu_parts(c):
    c2 = c * c
    t = jnp.tanh(SQRT_TWO_PI * (c * (1.0 + GELU_COEF * c2)))
    half = 0.5 * (1.0 + t)
    slope = half + 0.5 * c * (1.0 - t * t) * SQRT_TWO_PI * (1.0 + 3.0 * GELU_COEF * c2)
    return c * half, slope


def hidden_kernel(x_in, up, down, z_in,
                  h_out, dc_out, x_out, z_out, dx_own, dx_oth, up_d, up_x, up_xd, down_d, down_x, down_xd,
                  xv, zv, uv, vv, acc, h_st, dc_st,
                  act_send, act_recv, wx_send, wx_recv, wd_send, wd_recv, all_send, all_recv,
                  load_sem, local_sem, out_sem):
    cz, cy, cx = lax.axis_index("cz"), lax.axis_index("cy"), lax.axis_index("cx")
    to_x, to_y, to_d = {"cy": 1 - cy}, {"cz": 1 - cz}, {"cx": 1 - cx}
    rows, dk = x_in.shape
    ffc = up.shape[1]
    dq = down.shape[1]
    chunks = ffc // W

    def remote(src, dst, send, recv, dev):
        return pltpu.make_async_remote_copy(src_ref=src, dst_ref=dst, send_sem=send, recv_sem=recv,
                                            device_id=dev, device_id_type=MESH)

    def mine(c):
        return pl.ds(pl.multiple_of(c * W, W), W)

    def frow(f, c):
        return pl.ds(pl.multiple_of(f * ffc + c * W, W), W)

    own, oth = pl.ds(0, rows), pl.ds(rows, rows)
    near, far = pl.ds(0, dk), pl.ds(dk, dk)

    x1 = remote(x_in, xv.at[own, far], act_send.at[0], act_recv.at[0], to_x)
    z1 = remote(z_in, zv.at[own, far], act_send.at[1], act_recv.at[1], to_x)
    x2 = remote(x_in, xv.at[oth, near], act_send.at[2], act_recv.at[2], to_y)
    z2 = remote(z_in, zv.at[oth, near], act_send.at[3], act_recv.at[3], to_y)
    x3 = remote(xv.at[own, far], xv.at[oth, far], act_send.at[4], act_recv.at[4], to_y)
    z3 = remote(zv.at[own, far], zv.at[oth, far], act_send.at[5], act_recv.at[5], to_y)
    up_all = remote(up, up_d, all_send.at[0], all_recv.at[0], to_d)
    down_all = remote(down, down_d, all_send.at[1], all_recv.at[1], to_d)

    def over_x(c):
        return [remote(up.at[:, mine(c)], up_x.at[:, mine(c)], wx_send.at[c, 0], wx_recv.at[c, 0], to_x)] + [
            remote(down.at[frow(f, c)], down_x.at[frow(f, c)], wx_send.at[c, 1 + f], wx_recv.at[c, 1 + f], to_x)
            for f in range(2)]

    def over_d(c):
        return [remote(up_x.at[:, mine(c)], up_xd.at[:, mine(c)], wd_send.at[c, 0], wd_recv.at[c, 0], to_d)] + [
            remote(down_x.at[frow(f, c)], down_xd.at[frow(f, c)], wd_send.at[c, 1 + f], wd_recv.at[c, 1 + f], to_d)
            for f in range(2)]

    def lanes(part, core):
        return pl.ds(pl.multiple_of(part * dk + core * dq, 128), dq)

    def loads(c, late):
        slot = lax.rem(c, SLOTS)
        left, right = pl.ds(0, W), pl.ds(W, W)
        if late:
            moves = [(up_xd.at[:, mine(c)], uv.at[slot, far, right])]
            parts = [(down_xd, lanes(1, 1 - cx))]
        else:
            moves = [(up.at[:, mine(c)], uv.at[slot, near, left]),
                     (up_d.at[:, mine(c)], uv.at[slot, near, right]),
                     (up_x.at[:, mine(c)], uv.at[slot, far, left])]
            parts = [(down, lanes(0, cx)), (down_d, lanes(0, 1 - cx)), (down_x, lanes(1, cx))]
        for src, lane in parts:
            moves.append((src.at[frow(cx, c)], vv.at[slot, left, lane]))
            moves.append((src.at[frow(1 - cx, c)], vv.at[slot, right, lane]))
        base = 9 if late else 0
        return [pltpu.make_async_copy(s, d, load_sem.at[base + i]) for i, (s, d) in enumerate(moves)]

    barrier = pltpu.get_barrier_semaphore()
    for dev in (to_x, to_y, to_d):
        pl.semaphore_signal(barrier, inc=1, device_id=dev, device_id_type=MESH)
    pl.semaphore_wait(barrier, 3)

    x1.start()
    x2.start()
    z1.start()
    z2.start()
    for c in range(AHEAD):
        for copy in over_x(c):
            copy.start()
    up_all.start()
    down_all.start()
    x0 = pltpu.make_async_copy(x_in, xv.at[own, near], local_sem.at[0])
    z0 = pltpu.make_async_copy(z_in, zv.at[own, near], local_sem.at[1])
    x0.start()
    z0.start()

    @pl.loop(0, 2 * rows // 256)
    def _(i):
        acc[pl.ds(pl.multiple_of(i * 256, 256), 256), :] = jnp.zeros((256, dk), F32)

    x1.wait_recv()
    x3.start()
    z1.wait_recv()
    z3.start()
    x0.wait()
    z0.wait()
    up_all.wait_recv()
    down_all.wait_recv()
    x_save = pltpu.make_async_copy(xv.at[:, near], x_out, local_sem.at[0])
    z_save = pltpu.make_async_copy(zv.at[:, near], z_out, local_sem.at[1])

    def outs(n, c, r0):
        sl = lax.rem(n, 2)
        r = pl.ds(r0, RB)
        moves = []
        for k, (st, dst) in enumerate(((h_st, h_out), (dc_st, dc_out))):
            moves.append(pltpu.make_async_copy(st.at[sl, :, pl.ds(0, W)], dst.at[r, frow(cx, c)], out_sem.at[sl, 2 * k]))
            moves.append(pltpu.make_async_copy(st.at[sl, :, pl.ds(W, W)], dst.at[r, frow(1 - cx, c)], out_sem.at[sl, 2 * k + 1]))
        return moves

    nb = rows // RB
    steps = 2 * chunks

    @pl.loop(0, steps)
    def _(s):
        late = s >= 6
        c = jnp.where(late, 3 + (s - 6) // 2, lax.rem(s, 3))
        half = jnp.where(late, lax.rem(s, 2), s // 3)
        odd = lax.rem(s, 2) == 1
        hc = jnp.where(s < 3, s, 3 + (s - 5) // 2)

        @pl.when((s < 3) | ((s >= 5) & odd & (s < steps - 1)))
        def _():
            for copy in over_x(hc):
                copy.wait_recv()
            for copy in over_d(hc):
                copy.start()

            @pl.when(hc + AHEAD < chunks)
            def _():
                for copy in over_x(hc + AHEAD):
                    copy.start()

            for copy in loads(hc, False):
                copy.start()

        @pl.when((s < 3) | (late & ~odd))
        def _():
            for copy in over_d(c):
                copy.wait_recv()
            for copy in loads(c, True):
                copy.start()
            for copy in loads(c, False) + loads(c, True):
                copy.wait()

        @pl.when(s == 3)
        def _():
            x2.wait_recv()
            z2.wait_recv()
            x_save.start()
            z_save.start()
            x3.wait_recv()
            z3.wait_recv()

        slot = lax.rem(c, SLOTS)

        @pl.loop(0, nb)
        def _(b):
            r0 = pl.multiple_of(half * rows + b * RB, RB)
            n = s * nb + b
            sl = lax.rem(n, 2)
            cc = jnp.dot(xv[pl.ds(r0, RB), :], uv[slot], preferred_element_type=F32)
            dh = lax.dot_general(zv[pl.ds(r0, RB), :], vv[slot], LAST, preferred_element_type=F32)
            h, slope = gelu_parts(cc.astype(BF16).astype(F32))
            dc = (dh * slope).astype(BF16)

            @pl.when(n >= 2)
            def _():
                for copy in outs(n, c, r0):
                    copy.wait()

            h_st[sl] = h.astype(BF16)
            dc_st[sl] = dc
            for copy in outs(n, c, r0):
                copy.start()
            acc[pl.ds(r0, RB), :] += lax.dot_general(dc, uv[slot, near, :], LAST, preferred_element_type=F32)

    save = [pltpu.make_async_copy(acc.at[own], dx_own, load_sem.at[0]),
            pltpu.make_async_copy(acc.at[oth], dx_oth, load_sem.at[1])]
    for copy in save:
        copy.start()
    for n in range(2):
        for copy in outs(n, 0, 0):
            copy.wait()
    x_save.wait()
    z_save.wait()
    for copy in (x1, z1, x2, z2, x3, z3, up_all, down_all):
        copy.wait_send()

    @pl.loop(0, chunks)
    def _(c):
        for copy in over_x(c) + over_d(c):
            copy.wait_send()

    for copy in save:
        copy.wait()


def hidden_call(x_act, w_up, w_down, z_grad):
    rows, dk = x_act.shape
    ffc = w_up.shape[1]
    ff, _ = w_down.shape
    chunks = ffc // W
    flops = 2 * rows * 2 * ff * dk * 5
    hbm = pl.BlockSpec(memory_space=pl.ANY)
    sds = jax.ShapeDtypeStruct
    out_shape = [
        sds((2 * rows, ff), BF16), sds((2 * rows, ff), BF16),
        sds((2 * rows, dk), BF16), sds((2 * rows, dk), BF16),
        sds((rows, dk), F32), sds((rows, dk), F32),
        sds(w_up.shape, BF16), sds(w_up.shape, BF16), sds(w_up.shape, BF16),
        sds(w_down.shape, BF16), sds(w_down.shape, BF16), sds(w_down.shape, BF16),
    ]
    dma = pltpu.SemaphoreType.DMA
    return pl.pallas_call(
        hidden_kernel,
        in_specs=[hbm] * 4,
        out_specs=[hbm] * len(out_shape),
        out_shape=out_shape,
        scratch_shapes=[
            pltpu.VMEM((2 * rows, 2 * dk), BF16), pltpu.VMEM((2 * rows, 2 * dk), BF16),
            pltpu.VMEM((SLOTS, 2 * dk, 2 * W), BF16), pltpu.VMEM((SLOTS, 2 * W, 2 * dk), BF16),
            pltpu.VMEM((2 * rows, dk), F32),
            pltpu.VMEM((2, RB, 2 * W), BF16), pltpu.VMEM((2, RB, 2 * W), BF16),
            dma((6,)), dma((6,)), dma((chunks, 3)), dma((chunks, 3)), dma((chunks, 3)), dma((chunks, 3)),
            dma((2,)), dma((2,)), dma((12,)), dma((2,)), dma((2, 4)),
        ],
        compiler_params=pltpu.CompilerParams(
            collective_id=0, has_side_effects=True, vmem_limit_bytes=67_000_000),
        cost_estimate=pl.CostEstimate(flops=flops, bytes_accessed=200_000_000, transcendentals=2 * rows * ff),
        name="hidden",
    )(x_act, w_up, w_down, z_grad)


def solution(mesh):
    row_spec = P(("dp", "cx", "cz"), "cy")
    up_spec = P("cy", ("cz", "cx"))
    down_spec = P("cz", ("cy", "cx"))
    up_out = P(("dp", "cy"), ("cz", "cx"))
    down_out = P(("dp", "cz"), ("cy", "cx"))
    swap = [(0, 1), (1, 0)]

    def local_step(x_act, w_up, w_down, z_grad):
        h, dc, xs, zs, dx_own, dx_oth = hidden_call(x_act, w_up, w_down, z_grad)[:6]
        got = lax.ppermute(dx_oth, "cz", swap)
        down_part = lax.dot_general(h, zs, FIRST, preferred_element_type=F32)
        up_part = lax.dot_general(xs, dc, FIRST, preferred_element_type=F32)
        down_sum = lax.psum_scatter(down_part, "cx", scatter_dimension=1, tiled=True)
        up_sum = lax.psum_scatter(up_part, "cx", scatter_dimension=1, tiled=True)
        down_grad = down_sum.astype(BF16)
        up_grad = up_sum.astype(BF16)
        x_grad = (dx_own + got).astype(BF16)
        return (x_grad, up_grad, down_grad)

    return jax.shard_map(local_step, mesh=mesh, in_specs=(row_spec, up_spec, down_spec, row_spec), out_specs=(row_spec, up_out, down_out), check_vma=False)
```

time: 1830 us -> 650 us (0.36)
  waiting for transfers between devices: 1580 us -> 113 us
  Pallas kernels: 0 us -> 430 us
  matrix products: 175 us -> 70 us
  other arithmetic: 47.7 us -> 21 us
    unnamed x13 -> x2, waiting for transfers between devices: 886 us -> 0.03 us
    all_gather x6 -> x0, waiting for transfers between devices: 572 us -> none  [the longest x1 244 us: local_step(): grad_full = lax.all_gather(pre_grad, 'cy', axis=0, tiled=True)]
    pallas_call x0 -> x1, Pallas kernels: none -> 430 us  [hidden_call(): pl.pallas_call(hidden_kernel, in_specs=[hbm] * 4, out_specs=[hbm] * len(o...]
    ppermute x0 -> x1, waiting for transfers between devices: none -> 113 us  [local_step(): got = lax.ppermute(dx_oth, 'cz', swap)]
    reduce_scatter x2 -> x1, waiting for transfers between devices: 112 us -> 0.01 us  [local_step(): up_sum = lax.psum_scatter(up_part, 'cx', scatter_dimension=1, tiled=True)]
    dot_general x5 -> x2, matrix products: 175 us -> 70 us  [the longest x1 35.4 us: local_step(): down_part = lax.dot_general(h, zs, FIRST, preferred_element_type=F32)]
    convert_element_type x4 -> x3, other arithmetic: 47.7 us -> 21 us  [the longest x1 8.3 us: local_step(): up_grad = up_sum.astype(BF16)]
  transfers between devices with their start and end apart: 11 -> 3, of which waited for: 11 -> 1; matrix products, arithmetic and copies ran while one was open for 11% -> 7% of each run, Pallas kernels for 0% -> 0%
where the time goes in v1:
time: 650 us; the launch traced here: 649 us
  Pallas kernels  430 us (66%)
  waiting for transfers between devices  113 us (17%)
  matrix products  70 us (11%)
  other arithmetic  21 us (3%)
  between operations  14 us (2%)
    pallas_call x1, Pallas kernels, hidden_call(): pl.pallas_call(hidden_kernel, in_specs=[hbm] * 4, out_specs=[hbm] * len(o...  430 us
    ppermute x1, waiting for transfers between devices, local_step(): got = lax.ppermute(dx_oth, 'cz', swap)  113 us
    dot_general x1, matrix products, local_step(): down_part = lax.dot_general(h, zs, FIRST, preferred_element_type=F32)  35.4 us
    dot_general x1, matrix products, local_step(): up_part = lax.dot_general(xs, dc, FIRST, preferred_element_type=F32)  34.5 us
  transfers between devices with their start and end apart: 3, of which 1 were waited for; matrix products, arithmetic and copies ran while one was open for 7% of the time, Pallas kernels for 0%

profile of v1, /device:TPU:0, one launch (start us, length us, event | category | flops | bytes accessed | tf_op | source)
XLA Modules:
  0.0 649.0 jit_solution(8894876932645349629)
XLA Ops:
  7.2 0.0 reduce-scatter.3.cloned.1.call-start
  7.2 430.4 %hidden.1 = (bf16[2048,5120]{1,0:T(8,128)(2,1)}, bf16[2048,5120]{1,0:T(8,128)(2,1)}, bf16[2048,1280]{1,0:T(8,128)(2,1)}, bf16[2048,1280]{1,0:T(8,128)(2,1)}, f32...) custom-call(bf16[1024,1280]{1,0:T(8,128)(2,1)} %x_in.1, ...), custom_call_target="tpu_custom_call" | custom-call | flops 134217728000 | bytes 200000000 | tf_op jit(solution)/shard_map/hidden/pallas_call | solution.py:243
  437.6 34.5 %fusion = f32[1280,5120]{1,0:T(8,128)} fusion(bf16[2048,1280]{1,0:T(8,128)(2,1)} %get-tuple-element.11, bf16[2048,5120]{1,0:T(8,128)(2,1)} %get-tuple-element.12), kind=kOutput, calls=%fused_computation.1 | convolution fusion | flops 26843545600 | bytes 52428800 | tf_op jit(solution)/shard_map/dot_general | solution.py:275
  472.1 0.0 reduce-scatter.3.cloned.1.call-update
  472.2 0.2 reduce-scatter.5.cloned.1.call-start
  472.4 35.4 %fusion.1 = f32[5120,1280]{1,0:T(8,128)} fusion(bf16[2048,5120]{1,0:T(8,128)(2,1)} %get-tuple-element.13, bf16[2048,1280]{1,0:T(8,128)(2,1)} %get-tuple-element.14), kind=kOutput, calls=%fused_computation.2 | convolution fusion | flops 26843545600 | bytes 52428800 | tf_op jit(solution)/shard_map/dot_general | solution.py:274
  507.8 0.0 reduce-scatter.5.cloned.1.call-update
  507.9 0.2 collective-permute-start
  508.0 113.2 %collective-permute-done = f32[1024,1280]{1,0:T(8,128)S(1)} collective-permute-done((f32[1024,1280]{1,0:T(8,128)}, f32[1024,1280]{1,0:T(8,128)S(1)}, u32[]{:S(2)}, u32[]{:S(2)}) %collective-permute-start) | collective-permute-done | bytes 5242912 | tf_op jit(solution)/shard_map/ppermute | solution.py:273
  621.2 4.5 add_convert_fusion
  625.7 0.0 reduce-scatter.3.cloned.1.call-done
  625.7 8.3 %convert_element_type.10 = bf16[1280,2560]{1,0:T(8,128)(2,1)} convert(f32[1280,2560]{1,0:T(8,128)} %reduce-scatter.3.cloned.1.call-done) | non-fusion elementwise | flops 3276800 | bytes 19660800 | tf_op jit(solution)/shard_map/convert_element_type | solution.py:279
  634.0 0.0 reduce-scatter.5.cloned.1.call-done
  634.0 8.2 %convert_element_type.11 = bf16[5120,640]{1,0:T(8,128)(2,1)} convert(f32[5120,640]{1,0:T(8,128)} %reduce-scatter.5.cloned.1.call-done) | non-fusion elementwise | flops 3276800 | bytes 19660800 | tf_op jit(solution)/shard_map/convert_element_type | solution.py:278
Async XLA Ops:
  7.2 618.5 %reduce-scatter.3.cloned.1.call-start = ((), (), s32[]{:S(2)}) async-start(), calls=%async_computation.2 | async-start | bytes 39321600 | tf_op jit(solution)/shard_map/reduce_scatter | solution.py:277
  472.2 161.8 %reduce-scatter.5.cloned.1.call-start = ((), (), s32[]{:S(2)}) async-start(), calls=%async_computation.3 | async-start | bytes 39321600 | tf_op jit(solution)/shard_map/reduce_scatter | solution.py:276
  507.9 113.3 %collective-permute-start = (f32[1024,1280]{1,0:T(8,128)}, f32[1024,1280]{1,0:T(8,128)S(1)}, u32[]{:S(2)}, u32[]{:S(2)}) collective-permute-start(f32[1024,1280]{1,0:T(8,128)} %get-tuple-element.10), channel_id=1, source_target_pairs={{0,4},{4,0},{1,5},{5,1},{2,6},{6,2},{3,7},{7,3}} | collective-permute-start | bytes 15728648 | tf_op jit(solution)/shard_map/ppermute | solution.py:273
Sparse Core Ops, SparseCore 0:
  472.3 28.3 reduce-scatter.2
  508.0 27.4 reduce-scatter.4

commit v2 on v1

--- a/solution.py
+++ b/solution.py
@@ -15,10 +15,10 @@
 MESH = pl.DeviceIdType.MESH
 
 
-W = 256
-RB = 512
-AHEAD = 3
-SLOTS = 3
+W = 128
+RB = 1024
+AHEAD = 6
+SLOTS = 6
 
 
 def gelu_parts(c):
@@ -30,7 +30,7 @@
 
 
 def hidden_kernel(x_in, up, down, z_in,
-                  h_out, dc_out, x_out, z_out, dx_own, dx_oth, up_d, up_x, up_xd, down_d, down_x, down_xd,
+                  h_out, dc_own, dc_oth, x_out, z_own, z_oth, dx_own, dx_oth, up_d, up_x, up_xd, down_d, down_x, down_xd,
                   xv, zv, uv, vv, acc, h_st, dc_st,
                   act_send, act_recv, wx_send, wx_recv, wd_send, wd_recv, all_send, all_recv,
                   load_sem, local_sem, out_sem):
@@ -125,29 +125,29 @@
     up_all.wait_recv()
     down_all.wait_recv()
     x_save = pltpu.make_async_copy(xv.at[:, near], x_out, local_sem.at[0])
-    z_save = pltpu.make_async_copy(zv.at[:, near], z_out, local_sem.at[1])
+    z_save = [pltpu.make_async_copy(zv.at[:, lanes(0, cx)], z_own, local_sem.at[1]),
+              pltpu.make_async_copy(zv.at[:, lanes(0, 1 - cx)], z_oth, local_sem.at[2])]
 
     def outs(n, c, r0):
         sl = lax.rem(n, 2)
         r = pl.ds(r0, RB)
-        moves = []
-        for k, (st, dst) in enumerate(((h_st, h_out), (dc_st, dc_out))):
-            moves.append(pltpu.make_async_copy(st.at[sl, :, pl.ds(0, W)], dst.at[r, frow(cx, c)], out_sem.at[sl, 2 * k]))
-            moves.append(pltpu.make_async_copy(st.at[sl, :, pl.ds(W, W)], dst.at[r, frow(1 - cx, c)], out_sem.at[sl, 2 * k + 1]))
-        return moves
+        left, right = pl.ds(0, W), pl.ds(W, W)
+        moves = ((h_st.at[sl, :, left], h_out.at[r, frow(cx, c)]), (h_st.at[sl, :, right], h_out.at[r, frow(1 - cx, c)]),
+                 (dc_st.at[sl, :, left], dc_own.at[r, mine(c)]), (dc_st.at[sl, :, right], dc_oth.at[r, mine(c)]))
+        return [pltpu.make_async_copy(src, dst, out_sem.at[sl, i]) for i, (src, dst) in enumerate(moves)]
 
     nb = rows // RB
     steps = 2 * chunks
 
     @pl.loop(0, steps)
     def _(s):
-        late = s >= 6
-        c = jnp.where(late, 3 + (s - 6) // 2, lax.rem(s, 3))
-        half = jnp.where(late, lax.rem(s, 2), s // 3)
+        late = s >= 2 * SLOTS
+        c = jnp.where(late, SLOTS + (s - 2 * SLOTS) // 2, lax.rem(s, SLOTS))
+        half = jnp.where(late, lax.rem(s, 2), s // SLOTS)
         odd = lax.rem(s, 2) == 1
-        hc = jnp.where(s < 3, s, 3 + (s - 5) // 2)
-
-        @pl.when((s < 3) | ((s >= 5) & odd & (s < steps - 1)))
+        hc = jnp.where(s < SLOTS, s, SLOTS + (s - 2 * SLOTS + 1) // 2)
+
+        @pl.when((s < SLOTS) | ((s >= 2 * SLOTS - 1) & odd & (s < steps - 1)))
         def _():
             for copy in over_x(hc):
                 copy.wait_recv()
@@ -162,7 +162,7 @@
             for copy in loads(hc, False):
                 copy.start()
 
-        @pl.when((s < 3) | (late & ~odd))
+        @pl.when((s < SLOTS) | (late & ~odd))
         def _():
             for copy in over_d(c):
                 copy.wait_recv()
@@ -171,12 +171,13 @@
             for copy in loads(c, False) + loads(c, True):
                 copy.wait()
 
-        @pl.when(s == 3)
+        @pl.when(s == SLOTS)
         def _():
             x2.wait_recv()
             z2.wait_recv()
             x_save.start()
-            z_save.start()
+            for copy in z_save:
+                copy.start()
             x3.wait_recv()
             z3.wait_recv()
 
@@ -211,7 +212,8 @@
         for copy in outs(n, 0, 0):
             copy.wait()
     x_save.wait()
-    z_save.wait()
+    for copy in z_save:
+        copy.wait()
     for copy in (x1, z1, x2, z2, x3, z3, up_all, down_all):
         copy.wait_send()
 
@@ -227,14 +229,14 @@
 def hidden_call(x_act, w_up, w_down, z_grad):
     rows, dk = x_act.shape
     ffc = w_up.shape[1]
-    ff, _ = w_down.shape
+    ff, dq = w_down.shape
     chunks = ffc // W
     flops = 2 * rows * 2 * ff * dk * 5
     hbm = pl.BlockSpec(memory_space=pl.ANY)
     sds = jax.ShapeDtypeStruct
     out_shape = [
-        sds((2 * rows, ff), BF16), sds((2 * rows, ff), BF16),
-        sds((2 * rows, dk), BF16), sds((2 * rows, dk), BF16),
+        sds((2 * rows, ff), BF16), sds((2 * rows, ffc), BF16), sds((2 * rows, ffc), BF16),
+        sds((2 * rows, dk), BF16), sds((2 * rows, dq), BF16), sds((2 * rows, dq), BF16),
         sds((rows, dk), F32), sds((rows, dk), F32),
         sds(w_up.shape, BF16), sds(w_up.shape, BF16), sds(w_up.shape, BF16),
         sds(w_down.shape, BF16), sds(w_down.shape, BF16), sds(w_down.shape, BF16),
@@ -251,7 +253,7 @@
             pltpu.VMEM((2 * rows, dk), F32),
             pltpu.VMEM((2, RB, 2 * W), BF16), pltpu.VMEM((2, RB, 2 * W), BF16),
             dma((6,)), dma((6,)), dma((chunks, 3)), dma((chunks, 3)), dma((chunks, 3)), dma((chunks, 3)),
-            dma((2,)), dma((2,)), dma((12,)), dma((2,)), dma((2, 4)),
+            dma((2,)), dma((2,)), dma((12,)), dma((3,)), dma((2, 4)),
         ],
         compiler_params=pltpu.CompilerParams(
             collective_id=0, has_side_effects=True, vmem_limit_bytes=67_000_000),
@@ -269,14 +271,14 @@
     swap = [(0, 1), (1, 0)]
 
     def local_step(x_act, w_up, w_down, z_grad):
-        h, dc, xs, zs, dx_own, dx_oth = hidden_call(x_act, w_up, w_down, z_grad)[:6]
+        h, dc_own, dc_oth, xs, z_own, z_oth, dx_own, dx_oth = hidden_call(x_act, w_up, w_down, z_grad)[:8]
         got = lax.ppermute(dx_oth, "cz", swap)
-        down_part = lax.dot_general(h, zs, FIRST, preferred_element_type=F32)
-        up_part = lax.dot_general(xs, dc, FIRST, preferred_element_type=F32)
-        down_sum = lax.psum_scatter(down_part, "cx", scatter_dimension=1, tiled=True)
-        up_sum = lax.psum_scatter(up_part, "cx", scatter_dimension=1, tiled=True)
-        down_grad = down_sum.astype(BF16)
-        up_grad = up_sum.astype(BF16)
+        down_part = lax.dot_general(h, z_oth, FIRST, preferred_element_type=F32)
+        up_part = lax.dot_general(xs, dc_oth, FIRST, preferred_element_type=F32)
+        down_got = lax.ppermute(down_part, "cx", swap)
+        up_got = lax.ppermute(up_part, "cx", swap)
+        down_grad = (lax.dot_general(h, z_own, FIRST, preferred_element_type=F32) + down_got).astype(BF16)
+        up_grad = (lax.dot_general(xs, dc_own, FIRST, preferred_element_type=F32) + up_got).astype(BF16)
         x_grad = (dx_own + got).astype(BF16)
         return (x_grad, up_grad, down_grad)
 

time: 650 us -> 627 us (0.965)
  other arithmetic: 21 us -> 1.98 us
  matrix products: 70 us -> 87.5 us
  between operations: 14 us -> 0.68 us
  Pallas kernels: 430 us -> 420 us
    dot_general x2 -> x4, matrix products: 70 us -> 87.5 us  [the longest x1 25.1 us: local_step(): lax.dot_general(h, z_own, FIRST, preferred_element_type=F32) + down_got]
    convert_element_type x2 -> x0, other arithmetic: 16.5 us -> none  [the longest x1 8.3 us: local_step(): up_grad = up_sum.astype(BF16)]
    pallas_call x1, Pallas kernels: 430 us -> 420 us  [hidden_call(): pl.pallas_call(hidden_kernel, in_specs=[hbm] * 4, out_specs=[hbm] * len(o...]
where the time goes in v2:
time: 627 us; the launch traced here: 626 us
  Pallas kernels  420 us (67%)
  waiting for transfers between devices  114 us (18%)
  matrix products  87.5 us (14%)
    pallas_call x1, Pallas kernels, hidden_call(): pl.pallas_call(hidden_kernel, in_specs=[hbm] * 4, out_specs=[hbm] * len(o...  420 us
    ppermute x1, waiting for transfers between devices, local_step(): got = lax.ppermute(dx_oth, 'cz', swap)  114 us
    dot_general x1, matrix products, local_step(): lax.dot_general(h, z_own, FIRST, preferred_element_type=F32) + down_got  25.1 us
    dot_general x1, matrix products, local_step(): lax.dot_general(xs, dc_own, FIRST, preferred_element_type=F32) + up_got  22 us
    dot_general x1, matrix products, local_step(): down_part = lax.dot_general(h, z_oth, FIRST, preferred_element_type=F32)  20.7 us
    dot_general x1, matrix products, local_step(): up_part = lax.dot_general(xs, dc_oth, FIRST, preferred_element_type=F32)  19.6 us
  transfers between devices with their start and end apart: 3, of which 1 were waited for; matrix products, arithmetic and copies ran while one was open for 7% of the time, Pallas kernels for 0%

profile of v2, /device:TPU:0, one launch (start us, length us, event | category | flops | bytes accessed | tf_op | source)
XLA Modules:
  0.0 625.7 jit_solution(11478664283706532583)
XLA Ops:
  0.6 419.9 %hidden.1 = (bf16[2048,5120]{1,0:T(8,128)(2,1)}, bf16[2048,2560]{1,0:T(8,128)(2,1)}, bf16[2048,2560]{1,0:T(8,128)(2,1)}, bf16[2048,1280]{1,0:T(8,128)(2,1)}, bf1...) custom-call(bf16[1024,1280]{1,0:T(8,128)(2,1)} %x_in.1, ...), custom_call_target="tpu_custom_call" | custom-call | flops 134217728000 | bytes 200000000 | tf_op jit(solution)/shard_map/hidden/pallas_call | solution.py:245
  420.5 0.0 copy-start.1
  420.5 20.7 %fusion.2 = f32[5120,640]{1,0:T(8,128)S(1)} fusion(bf16[2048,5120]{1,0:T(8,128)(2,1)} %get-tuple-element.16, bf16[2048,640]{1,0:T(8,128)(2,1)} %get-tuple-element.18), kind=kOutput, calls=%fused_computation.5 | convolution fusion | flops 13421772800 | bytes 36700160 | tf_op jit(solution)/shard_map/dot_general | solution.py:276
  441.2 0.0 collective-permute-start.2
  441.2 0.0 copy-done.1
  441.3 0.0 copy-start
  441.3 19.6 %fusion.1 = f32[1280,2560]{1,0:T(8,128)} fusion(bf16[2048,1280]{1,0:T(8,128)(2,1)S(1)} %copy-done.1, bf16[2048,2560]{1,0:T(8,128)(2,1)} %get-tuple-element.15), kind=kOutput, calls=%fused_computation.4 | convolution fusion | flops 13421772800 | bytes 28835840 | tf_op jit(solution)/shard_map/dot_general | solution.py:277
  460.9 0.3 collective-permute-start.1
  461.2 1.0 collective-permute-start
  462.2 114.4 %collective-permute-done = f32[1024,1280]{1,0:T(8,128)S(1)} collective-permute-done((f32[1024,1280]{1,0:T(8,128)}, f32[1024,1280]{1,0:T(8,128)S(1)}, u32[]{:S(2)}, u32[]{:S(2)}) %collective-permute-start) | collective-permute-done | bytes 5242912 | tf_op jit(solution)/shard_map/ppermute | solution.py:275
  576.6 0.0 copy-done
  576.6 2.0 add_convert_fusion.1
  578.6 0.0 collective-permute-done.2
  578.6 25.1 %add_convert_fusion = bf16[5120,640]{1,0:T(8,128)(2,1)} fusion(f32[5120,640]{1,0:T(8,128)} %collective-permute-done.2, bf16[2048,5120]{1,0:T(8,128)(2,1)} %get-tuple-element.16, bf16[2048,640]{1,0:T(8,128)(2,1)} %get-tuple-element.17), kind=kOutput, calls=%fused_computation.1 | convolution fusion | flops 13428326400 | bytes 43253760 | tf_op jit(solution)/shard_map/dot_general | solution.py:280
  603.7 0.0 collective-permute-done.1
  603.7 22.0 %fusion = bf16[1280,2560]{1,0:T(8,128)(2,1)} fusion(f32[1280,2560]{1,0:T(8,128)} %collective-permute-done.1, bf16[2048,1280]{1,0:T(8,128)(2,1)} %get-tuple-element.13, bf16[2048,2560]{1,0:T(8,128)(2,1)} %get-tuple-element.14), kind=kOutput, calls=%fused_computation.2 | convolution fusion | flops 13428326400 | bytes 35389440 | tf_op jit(solution)/shard_map/dot_general | solution.py:281
Async XLA Ops:
  420.5 20.8 %copy-start.1 = (bf16[2048,1280]{1,0:T(8,128)(2,1)S(1)}, bf16[2048,1280]{1,0:T(8,128)(2,1)}, u32[]{:S(2)}) copy-start(bf16[2048,1280]{1,0:T(8,128)(2,1)} %get-tuple-element.13) | copy-start | bytes 15728644
  441.2 137.4 %collective-permute-start.2 = (f32[5120,640]{1,0:T(8,128)S(1)}, f32[5120,640]{1,0:T(8,128)}, u32[]{:S(2)}, u32[]{:S(2)}) collective-permute-start(f32[5120,640]{1,0:T(8,128)S(1)} %fusion.2), channel_id=1, source_target_pairs={{0,1},{1,0},{2,3},{3,2},{4,5},{5,4},{6,7},{7,6}} | collective-permute-start | bytes 39321608 | tf_op jit(solution)/shard_map/ppermute | solution.py:278
  441.3 135.3 %copy-start = (f32[1024,1280]{1,0:T(8,128)S(1)}, f32[1024,1280]{1,0:T(8,128)}, u32[]{:S(2)}) copy-start(f32[1024,1280]{1,0:T(8,128)} %get-tuple-element.11) | copy-start | bytes 15728644
  460.9 142.8 %collective-permute-start.1 = (f32[1280,2560]{1,0:T(8,128)}, f32[1280,2560]{1,0:T(8,128)}, u32[]{:S(2)}, u32[]{:S(2)}) collective-permute-start(f32[1280,2560]{1,0:T(8,128)} %fusion.1), channel_id=1, source_target_pairs={{0,1},{1,0},{2,3},{3,2},{4,5},{5,4},{6,7},{7,6}} | collective-permute-start | bytes 39321608 | tf_op jit(solution)/shard_map/ppermute | solution.py:279
  461.2 115.4 %collective-permute-start = (f32[1024,1280]{1,0:T(8,128)}, f32[1024,1280]{1,0:T(8,128)S(1)}, u32[]{:S(2)}, u32[]{:S(2)}) collective-permute-start(f32[1024,1280]{1,0:T(8,128)} %get-tuple-element.12), channel_id=1, source_target_pairs={{0,4},{4,0},{1,5},{5,1},{2,6},{6,2},{3,7},{7,3}} | collective-permute-start | bytes 15728648 | tf_op jit(solution)/shard_map/ppermute | solution.py:275

commit v3 on v2

--- a/solution.py
+++ b/solution.py
@@ -17,6 +17,7 @@
 
 W = 128
 RB = 1024
+PHI = 8
 AHEAD = 6
 SLOTS = 6
 
@@ -30,10 +31,10 @@
 
 
 def hidden_kernel(x_in, up, down, z_in,
-                  h_out, dc_own, dc_oth, x_out, z_own, z_oth, dx_own, dx_oth, up_d, up_x, up_xd, down_d, down_x, down_xd,
+                  h_out, dc_own, dc_oth, x_out, z_own, z_oth, dx_own, dx_part, dx_got, dcp_own, dcp_oth, up_y, up_yd, up_d, up_x, up_xd, down_d, down_x, down_xd,
                   xv, zv, uv, vv, acc, h_st, dc_st,
                   act_send, act_recv, wx_send, wx_recv, wd_send, wd_recv, all_send, all_recv,
-                  load_sem, local_sem, out_sem):
+                  load_sem, local_sem, out_sem, extra_sem):
     cz, cy, cx = lax.axis_index("cz"), lax.axis_index("cy"), lax.axis_index("cx")
     to_x, to_y, to_d = {"cy": 1 - cy}, {"cz": 1 - cz}, {"cx": 1 - cx}
     rows, dk = x_in.shape
@@ -62,6 +63,14 @@
     z3 = remote(zv.at[own, far], zv.at[oth, far], act_send.at[5], act_recv.at[5], to_y)
     up_all = remote(up, up_d, all_send.at[0], all_recv.at[0], to_d)
     down_all = remote(down, down_d, all_send.at[1], all_recv.at[1], to_d)
+
+    split = chunks - PHI
+    tail = pl.ds(split * W, PHI * W)
+    up_tail = remote(up.at[:, tail], up_y, all_send.at[2], all_recv.at[2], to_y)
+    up_tail_d = remote(up_y, up_yd, all_send.at[3], all_recv.at[3], to_d)
+    part_save = pltpu.make_async_copy(acc.at[oth], dx_part, local_sem.at[3])
+    part_send = remote(dx_part, dx_got, all_send.at[4], all_recv.at[4], to_y)
+    own_save = pltpu.make_async_copy(acc.at[own], dx_own, local_sem.at[4])
 
     def over_x(c):
         return [remote(up.at[:, mine(c)], up_x.at[:, mine(c)], wx_send.at[c, 0], wx_recv.at[c, 0], to_x)] + [
@@ -120,6 +129,7 @@
     x3.start()
     z1.wait_recv()
     z3.start()
+    up_tail.start()
     x0.wait()
     z0.wait()
     up_all.wait_recv()
@@ -136,7 +146,12 @@
                  (dc_st.at[sl, :, left], dc_own.at[r, mine(c)]), (dc_st.at[sl, :, right], dc_oth.at[r, mine(c)]))
         return [pltpu.make_async_copy(src, dst, out_sem.at[sl, i]) for i, (src, dst) in enumerate(moves)]
 
-    nb = rows // RB
+    def extra(n, c):
+        sl = lax.rem(n, 2)
+        cols = pl.ds(pl.multiple_of((c - split) * W, W), W)
+        return [pltpu.make_async_copy(dc_st.at[sl, :, pl.ds(0, W)], dcp_own.at[:, cols], extra_sem.at[0]),
+                pltpu.make_async_copy(dc_st.at[sl, :, pl.ds(W, W)], dcp_oth.at[:, cols], extra_sem.at[1])]
+
     steps = 2 * chunks
 
     @pl.loop(0, steps)
@@ -181,49 +196,68 @@
             x3.wait_recv()
             z3.wait_recv()
 
+        @pl.when(s == 2 * split)
+        def _():
+            part_save.start()
+            up_tail.wait_recv()
+            up_tail_d.start()
+            part_save.wait()
+            part_send.start()
+
+        @pl.when(s == steps - 1)
+        def _():
+            own_save.start()
+
         slot = lax.rem(c, SLOTS)
-
-        @pl.loop(0, nb)
-        def _(b):
-            r0 = pl.multiple_of(half * rows + b * RB, RB)
-            n = s * nb + b
-            sl = lax.rem(n, 2)
-            cc = jnp.dot(xv[pl.ds(r0, RB), :], uv[slot], preferred_element_type=F32)
-            dh = lax.dot_general(zv[pl.ds(r0, RB), :], vv[slot], LAST, preferred_element_type=F32)
-            h, slope = gelu_parts(cc.astype(BF16).astype(F32))
-            dc = (dh * slope).astype(BF16)
-
-            @pl.when(n >= 2)
-            def _():
-                for copy in outs(n, c, r0):
-                    copy.wait()
-
-            h_st[sl] = h.astype(BF16)
-            dc_st[sl] = dc
-            for copy in outs(n, c, r0):
-                copy.start()
-            acc[pl.ds(r0, RB), :] += lax.dot_general(dc, uv[slot, near, :], LAST, preferred_element_type=F32)
-
-    save = [pltpu.make_async_copy(acc.at[own], dx_own, load_sem.at[0]),
-            pltpu.make_async_copy(acc.at[oth], dx_oth, load_sem.at[1])]
-    for copy in save:
-        copy.start()
+        r0 = pl.multiple_of(half * rows, RB)
+        sl = lax.rem(s, 2)
+        cc = jnp.dot(xv[pl.ds(r0, RB), :], uv[slot], preferred_element_type=F32)
+        dh = lax.dot_general(zv[pl.ds(r0, RB), :], vv[slot], LAST, preferred_element_type=F32)
+        h, slope = gelu_parts(cc.astype(BF16).astype(F32))
+        dc = (dh * slope).astype(BF16)
+
+        @pl.when(s >= 2)
+        def _():
+            for copy in outs(s, c, r0):
+                copy.wait()
+
+        @pl.when((s >= 2 * split + 3) & odd)
+        def _():
+            for copy in extra(s, c):
+                copy.wait()
+
+        h_st[sl] = h.astype(BF16)
+        dc_st[sl] = dc
+        for copy in outs(s, c, r0):
+            copy.start()
+
+        @pl.when((half == 0) | (c < split))
+        def _():
+            acc[pl.ds(r0, RB), :] += lax.dot_general(dc_st[sl], uv[slot, near, :], LAST, preferred_element_type=F32)
+
+        @pl.when((half == 1) & (c >= split))
+        def _():
+            for copy in extra(s, c):
+                copy.start()
+
     for n in range(2):
         for copy in outs(n, 0, 0):
             copy.wait()
+    for copy in extra(1, split):
+        copy.wait()
+    own_save.wait()
+    up_tail_d.wait_recv()
+    part_send.wait_recv()
     x_save.wait()
     for copy in z_save:
         copy.wait()
-    for copy in (x1, z1, x2, z2, x3, z3, up_all, down_all):
+    for copy in (x1, z1, x2, z2, x3, z3, up_all, down_all, up_tail, up_tail_d, part_send):
         copy.wait_send()
 
     @pl.loop(0, chunks)
     def _(c):
         for copy in over_x(c) + over_d(c):
             copy.wait_send()
-
-    for copy in save:
-        copy.wait()
 
 
 def hidden_call(x_act, w_up, w_down, z_grad):
@@ -237,7 +271,8 @@
     out_shape = [
         sds((2 * rows, ff), BF16), sds((2 * rows, ffc), BF16), sds((2 * rows, ffc), BF16),
         sds((2 * rows, dk), BF16), sds((2 * rows, dq), BF16), sds((2 * rows, dq), BF16),
-        sds((rows, dk), F32), sds((rows, dk), F32),
+        sds((rows, dk), F32), sds((rows, dk), F32), sds((rows, dk), F32),
+        sds((rows, PHI * W), BF16), sds((rows, PHI * W), BF16), sds((dk, PHI * W), BF16), sds((dk, PHI * W), BF16),
         sds(w_up.shape, BF16), sds(w_up.shape, BF16), sds(w_up.shape, BF16),
         sds(w_down.shape, BF16), sds(w_down.shape, BF16), sds(w_down.shape, BF16),
     ]
@@ -253,7 +288,7 @@
             pltpu.VMEM((2 * rows, dk), F32),
             pltpu.VMEM((2, RB, 2 * W), BF16), pltpu.VMEM((2, RB, 2 * W), BF16),
             dma((6,)), dma((6,)), dma((chunks, 3)), dma((chunks, 3)), dma((chunks, 3)), dma((chunks, 3)),
-            dma((2,)), dma((2,)), dma((12,)), dma((3,)), dma((2, 4)),
+            dma((5,)), dma((5,)), dma((12,)), dma((5,)), dma((2, 4)), dma((2,)),
         ],
         compiler_params=pltpu.CompilerParams(
             collective_id=0, has_side_effects=True, vmem_limit_bytes=67_000_000),
@@ -271,15 +306,18 @@
     swap = [(0, 1), (1, 0)]
 
     def local_step(x_act, w_up, w_down, z_grad):
-        h, dc_own, dc_oth, xs, z_own, z_oth, dx_own, dx_oth = hidden_call(x_act, w_up, w_down, z_grad)[:8]
-        got = lax.ppermute(dx_oth, "cz", swap)
+        (h, dc_own, dc_oth, xs, z_own, z_oth, dx_own, _, dx_got, dcp_own, dcp_oth, up_y, up_yd) = hidden_call(
+            x_act, w_up, w_down, z_grad)[:13]
+        dcr_own = lax.ppermute(dcp_own, "cz", swap)
+        dcr_oth = lax.ppermute(dcp_oth, "cz", swap)
         down_part = lax.dot_general(h, z_oth, FIRST, preferred_element_type=F32)
         up_part = lax.dot_general(xs, dc_oth, FIRST, preferred_element_type=F32)
         down_got = lax.ppermute(down_part, "cx", swap)
         up_got = lax.ppermute(up_part, "cx", swap)
         down_grad = (lax.dot_general(h, z_own, FIRST, preferred_element_type=F32) + down_got).astype(BF16)
         up_grad = (lax.dot_general(xs, dc_own, FIRST, preferred_element_type=F32) + up_got).astype(BF16)
-        x_grad = (dx_own + got).astype(BF16)
+        dx = lax.dot_general(dcr_own, up_y, LAST, preferred_element_type=F32) + (dx_own + dx_got)
+        x_grad = (lax.dot_general(dcr_oth, up_yd, LAST, preferred_element_type=F32) + dx).astype(BF16)
         return (x_grad, up_grad, down_grad)
 
     return jax.shard_map(local_step, mesh=mesh, in_specs=(row_spec, up_spec, down_spec, row_spec), out_specs=(row_spec, up_out, down_out), check_vma=False)

time: 627 us -> 626 us (level)
  waiting for transfers between devices: 114 us -> 84 us
  matrix products: 87.5 us -> 103 us
  Pallas kernels: 420 us -> 435 us
    ppermute x1 -> x2, waiting for transfers between devices: 114 us -> 83.9 us  [the longest x1 46.5 us: local_step(): dcr_own = lax.ppermute(dcp_own, 'cz', swap)]
    pallas_call x1, Pallas kernels: 420 us -> 435 us  [hidden_call(): pl.pallas_call(hidden_kernel, in_specs=[hbm] * 4, out_specs=[hbm] * len(o...]
    dot_general x0 -> x2, matrix products: none -> 14.5 us  [the longest x1 7.95 us: local_step(): lax.dot_general(dcr_oth, up_yd, LAST, preferred_element_type=F32) + dx]
  transfers between devices with their start and end apart: 3 -> 4, of which waited for: 1 -> 2; matrix products, arithmetic and copies ran while one was open for 7% -> 10% of each run, Pallas kernels for 0% -> 0%
where the time goes in v3:
time: 626 us
  Pallas kernels  435 us (69%)
  matrix products  103 us (16%)
  waiting for transfers between devices  84 us (13%)
    pallas_call x1, Pallas kernels, hidden_call(): pl.pallas_call(hidden_kernel, in_specs=[hbm] * 4, out_specs=[hbm] * len(o...  435 us
    ppermute x1, waiting for transfers between devices, local_step(): dcr_own = lax.ppermute(dcp_own, 'cz', swap)  46.5 us
    ppermute x1, waiting for transfers between devices, local_step(): dcr_oth = lax.ppermute(dcp_oth, 'cz', swap)  37.5 us
    dot_general x1, matrix products, local_step(): lax.dot_general(h, z_own, FIRST, preferred_element_type=F32) + down_got  25.5 us
    dot_general x1, matrix products, local_step(): lax.dot_general(xs, dc_own, FIRST, preferred_element_type=F32) + up_got  22 us
    dot_general x1, matrix products, local_step(): down_part = lax.dot_general(h, z_oth, FIRST, preferred_element_type=F32)  21.3 us
    dot_general x1, matrix products, local_step(): up_part = lax.dot_general(xs, dc_oth, FIRST, preferred_element_type=F32)  19.9 us
  transfers between devices with their start and end apart: 4, of which 2 were waited for; matrix products, arithmetic and copies ran while one was open for 10% of the time, Pallas kernels for 0%

profile of v3, /device:TPU:0, one launch (start us, length us, event | category | flops | bytes accessed | tf_op | source)
XLA Modules:
  0.0 625.6 jit_solution(262832692487200964)
XLA Ops:
  0.6 435.2 %hidden.1 = (bf16[2048,5120]{1,0:T(8,128)(2,1)}, bf16[2048,2560]{1,0:T(8,128)(2,1)}, bf16[2048,2560]{1,0:T(8,128)(2,1)}, bf16[2048,1280]{1,0:T(8,128)(2,1)}, bf1...) custom-call(bf16[1024,1280]{1,0:T(8,128)(2,1)} %x_in.1, ...), custom_call_target="tpu_custom_call" | custom-call | flops 134217728000 | bytes 200000000 | tf_op jit(solution)/shard_map/hidden/pallas_call | solution.py:280
  435.8 0.0 copy-start.3
  435.9 21.3 %fusion.3 = f32[5120,640]{1,0:T(8,128)S(1)} fusion(bf16[2048,5120]{1,0:T(8,128)(2,1)} %get-tuple-element.24, bf16[2048,640]{1,0:T(8,128)(2,1)} %get-tuple-element.26), kind=kOutput, calls=%fused_computation.6 | convolution fusion | flops 13421772800 | bytes 36700160 | tf_op jit(solution)/shard_map/dot_general | solution.py:313
  457.1 0.0 collective-permute-start.3
  457.2 0.0 copy-done.3
  457.2 0.0 copy-start.1
  457.2 0.0 copy-start
  457.2 19.9 %fusion.2 = f32[1280,2560]{1,0:T(8,128)} fusion(bf16[2048,1280]{1,0:T(8,128)(2,1)S(1)} %copy-done.3, bf16[2048,2560]{1,0:T(8,128)(2,1)} %get-tuple-element.23), kind=kOutput, calls=%fused_computation.5 | convolution fusion | flops 13421772800 | bytes 28835840 | tf_op jit(solution)/shard_map/dot_general | solution.py:314
  477.1 0.5 collective-permute-start.2
  477.6 0.0 copy-done.1
  477.6 1.5 collective-permute-start.1
  479.1 0.0 copy-done
  479.1 0.5 collective-permute-start
  479.6 46.5 %collective-permute-done.1 = bf16[1024,1024]{1,0:T(8,128)(2,1)S(1)} collective-permute-done((bf16[1024,1024]{1,0:T(8,128)(2,1)S(1)}, bf16[1024,1024]{1,0:T(8,128)(2,1)S(1)}, u32[]{:S(2)}, u32[]{:S(2)}) %collective-permute-start.1) | collective-permute-done | bytes 2097184 | tf_op jit(solution)/shard_map/ppermute | solution.py:311
  526.1 0.0 copy-start.2
  526.1 6.5 %fusion.1 = f32[1024,1280]{1,0:T(8,128)} fusion(bf16[1024,1024]{1,0:T(8,128)(2,1)S(1)} %collective-permute-done.1, bf16[1280,1024]{1,0:T(8,128)(2,1)} %get-tuple-element.18), kind=kOutput, calls=%fused_computation.4 | convolution fusion | flops 2684354560 | bytes 9961472 | tf_op jit(solution)/shard_map/dot_general | solution.py:319
  532.6 37.5 %collective-permute-done = bf16[1024,1024]{1,0:T(8,128)(2,1)S(1)} collective-permute-done((bf16[1024,1024]{1,0:T(8,128)(2,1)S(1)}, bf16[1024,1024]{1,0:T(8,128)(2,1)S(1)}, u32[]{:S(2)}, u32[]{:S(2)}) %collective-permute-start) | collective-permute-done | bytes 2097184 | tf_op jit(solution)/shard_map/ppermute | solution.py:312
  570.1 0.0 copy-done.2
  570.1 8.0 %add_convert_fusion.1 = bf16[1024,1280]{1,0:T(8,128)(2,1)} fusion(f32[1024,1280]{1,0:T(8,128)} %fusion.1, f32[1024,1280]{1,0:T(8,128)S(1)} %copy-done.2, f32[1024,1280]{1,0:T(8,128)} %get-tuple-element.20, bf16[1024,1024]{1,0:T(8,128)(2,1)S(1)} %collective-permute-done, bf16[1280,1024]{1,0:T(8,128)(2,1)} %get-tuple-element.16), kind=kOutput, calls=%fused_computation.3 | convolution fusion | flops 2689597440 | bytes 23068672 | tf_op jit(solution)/shard_map/dot_general | solution.py:320
  578.1 0.0 collective-permute-done.3
  578.1 25.5 %add_convert_fusion = bf16[5120,640]{1,0:T(8,128)(2,1)} fusion(f32[5120,640]{1,0:T(8,128)} %collective-permute-done.3, bf16[2048,5120]{1,0:T(8,128)(2,1)} %get-tuple-element.24, bf16[2048,640]{1,0:T(8,128)(2,1)} %get-tuple-element.25), kind=kOutput, calls=%fused_computation.1 | convolution fusion | flops 13428326400 | bytes 43253760 | tf_op jit(solution)/shard_map/dot_general | solution.py:317
  603.6 0.0 collective-permute-done.2
  603.6 22.0 %fusion = bf16[1280,2560]{1,0:T(8,128)(2,1)} fusion(f32[1280,2560]{1,0:T(8,128)} %collective-permute-done.2, bf16[2048,1280]{1,0:T(8,128)(2,1)} %get-tuple-element.21, bf16[2048,2560]{1,0:T(8,128)(2,1)} %get-tuple-element.22), kind=kOutput, calls=%fused_computation.2 | convolution fusion | flops 13428326400 | bytes 35389440 | tf_op jit(solution)/shard_map/dot_general | solution.py:318
Async XLA Ops:
  435.8 21.3 %copy-start.3 = (bf16[2048,1280]{1,0:T(8,128)(2,1)S(1)}, bf16[2048,1280]{1,0:T(8,128)(2,1)}, u32[]{:S(2)}) copy-start(bf16[2048,1280]{1,0:T(8,128)(2,1)} %get-tuple-element.21) | copy-start | bytes 15728644
  457.1 120.9 %collective-permute-start.3 = (f32[5120,640]{1,0:T(8,128)S(1)}, f32[5120,640]{1,0:T(8,128)}, u32[]{:S(2)}, u32[]{:S(2)}) collective-permute-start(f32[5120,640]{1,0:T(8,128)S(1)} %fusion.3), channel_id=1, source_target_pairs={{0,1},{1,0},{2,3},{3,2},{4,5},{5,4},{6,7},{7,6}} | collective-permute-start | bytes 39321608 | tf_op jit(solution)/shard_map/ppermute | solution.py:315
  457.2 20.4 %copy-start.1 = (bf16[1024,1024]{1,0:T(8,128)(2,1)S(1)}, bf16[1024,1024]{1,0:T(8,128)(2,1)}, u32[]{:S(2)}) copy-start(bf16[1024,1024]{1,0:T(8,128)(2,1)} %get-tuple-element.17) | copy-start | bytes 6291460
  457.2 21.9 %copy-start = (bf16[1024,1024]{1,0:T(8,128)(2,1)S(1)}, bf16[1024,1024]{1,0:T(8,128)(2,1)}, u32[]{:S(2)}) copy-start(bf16[1024,1024]{1,0:T(8,128)(2,1)} %get-tuple-element.15) | copy-start | bytes 6291460
  477.1 126.5 %collective-permute-start.2 = (f32[1280,2560]{1,0:T(8,128)}, f32[1280,2560]{1,0:T(8,128)}, u32[]{:S(2)}, u32[]{:S(2)}) collective-permute-start(f32[1280,2560]{1,0:T(8,128)} %fusion.2), channel_id=1, source_target_pairs={{0,1},{1,0},{2,3},{3,2},{4,5},{5,4},{6,7},{7,6}} | collective-permute-start | bytes 39321608 | tf_op jit(solution)/shard_map/ppermute | solution.py:316
  477.6 48.5 %collective-permute-start.1 = (bf16[1024,1024]{1,0:T(8,128)(2,1)S(1)}, bf16[1024,1024]{1,0:T(8,128)(2,1)S(1)}, u32[]{:S(2)}, u32[]{:S(2)}) collective-permute-start(bf16[1024,1024]{1,0:T(8,128)(2,1)S(1)} %copy-done.1), channel_id=1, source_target_pairs={{0,4},{4,0},{1,5},{5,1},{2,6},{6,2},{3,7},{7,3}} | collective-permute-start | bytes 6291464 | tf_op jit(solution)/shard_map/ppermute | solution.py:311
  479.1 91.0 %collective-permute-start = (bf16[1024,1024]{1,0:T(8,128)(2,1)S(1)}, bf16[1024,1024]{1,0:T(8,128)(2,1)S(1)}, u32[]{:S(2)}, u32[]{:S(2)}) collective-permute-start(bf16[1024,1024]{1,0:T(8,128)(2,1)S(1)} %copy-done), channel_id=1, source_target_pairs={{0,4},{4,0},{1,5},{5,1},{2,6},{6,2},{3,7},{7,3}} | collective-permute-start | bytes 6291464 | tf_op jit(solution)/shard_map/ppermute | solution.py:312
  526.1 44.0 %copy-start.2 = (f32[1024,1280]{1,0:T(8,128)S(1)}, f32[1024,1280]{1,0:T(8,128)}, u32[]{:S(2)}) copy-start(f32[1024,1280]{1,0:T(8,128)} %get-tuple-element.19) | copy-start | bytes 15728644

commit v4 on v3

--- a/solution.py
+++ b/solution.py
@@ -18,8 +18,8 @@
 W = 128
 RB = 1024
 PHI = 8
-AHEAD = 6
-SLOTS = 6
+AHEAD = 8
+SLOTS = 8
 
 
 def gelu_parts(c):
@@ -158,51 +158,51 @@
     def _(s):
         late = s >= 2 * SLOTS
         c = jnp.where(late, SLOTS + (s - 2 * SLOTS) // 2, lax.rem(s, SLOTS))
-        half = jnp.where(late, lax.rem(s, 2), s // SLOTS)
+        half = jnp.where(late, jnp.where(c < split, 1 - lax.rem(s, 2), lax.rem(s, 2)), s // SLOTS)
         odd = lax.rem(s, 2) == 1
         hc = jnp.where(s < SLOTS, s, SLOTS + (s - 2 * SLOTS + 1) // 2)
 
-        @pl.when((s < SLOTS) | ((s >= 2 * SLOTS - 1) & odd & (s < steps - 1)))
-        def _():
-            for copy in over_x(hc):
-                copy.wait_recv()
-            for copy in over_d(hc):
-                copy.start()
-
-            @pl.when(hc + AHEAD < chunks)
-            def _():
-                for copy in over_x(hc + AHEAD):
-                    copy.start()
-
-            for copy in loads(hc, False):
-                copy.start()
-
-        @pl.when((s < SLOTS) | (late & ~odd))
-        def _():
-            for copy in over_d(c):
-                copy.wait_recv()
-            for copy in loads(c, True):
-                copy.start()
-            for copy in loads(c, False) + loads(c, True):
-                copy.wait()
-
-        @pl.when(s == SLOTS)
-        def _():
-            x2.wait_recv()
-            z2.wait_recv()
-            x_save.start()
-            for copy in z_save:
-                copy.start()
-            x3.wait_recv()
-            z3.wait_recv()
-
-        @pl.when(s == 2 * split)
+        @pl.when(s == 2 * split - 1)
         def _():
             part_save.start()
             up_tail.wait_recv()
             up_tail_d.start()
             part_save.wait()
             part_send.start()
+
+        @pl.when((s < SLOTS) | ((s >= 2 * SLOTS - 1) & odd & (s < steps - 1)))
+        def _():
+            for copy in over_x(hc):
+                copy.wait_recv()
+            for copy in over_d(hc):
+                copy.start()
+
+            @pl.when(hc + AHEAD < chunks)
+            def _():
+                for copy in over_x(hc + AHEAD):
+                    copy.start()
+
+            for copy in loads(hc, False):
+                copy.start()
+
+        @pl.when((s < SLOTS) | (late & ~odd))
+        def _():
+            for copy in over_d(c):
+                copy.wait_recv()
+            for copy in loads(c, True):
+                copy.start()
+            for copy in loads(c, False) + loads(c, True):
+                copy.wait()
+
+        @pl.when(s == SLOTS)
+        def _():
+            x2.wait_recv()
+            z2.wait_recv()
+            x_save.start()
+            for copy in z_save:
+                copy.start()
+            x3.wait_recv()
+            z3.wait_recv()
 
         @pl.when(s == steps - 1)
         def _():

time: 626 us -> 619 us (0.989)
  Pallas kernels: 435 us -> 427 us
    pallas_call x1, Pallas kernels: 435 us -> 427 us  [hidden_call(): pl.pallas_call(hidden_kernel, in_specs=[hbm] * 4, out_specs=[hbm] * len(o...]
where the time goes in v4:
time: 619 us; the launch traced here: 618 us
  Pallas kernels  427 us (69%)
  matrix products  103 us (17%)
  waiting for transfers between devices  84.4 us (14%)
    pallas_call x1, Pallas kernels, hidden_call(): pl.pallas_call(hidden_kernel, in_specs=[hbm] * 4, out_specs=[hbm] * len(o...  427 us
    ppermute x1, waiting for transfers between devices, local_step(): dcr_own = lax.ppermute(dcp_own, 'cz', swap)  46.5 us
    ppermute x1, waiting for transfers between devices, local_step(): dcr_oth = lax.ppermute(dcp_oth, 'cz', swap)  37.9 us
    dot_general x1, matrix products, local_step(): lax.dot_general(h, z_own, FIRST, preferred_element_type=F32) + down_got  25.5 us
    dot_general x1, matrix products, local_step(): lax.dot_general(xs, dc_own, FIRST, preferred_element_type=F32) + up_got  22 us
    dot_general x1, matrix products, local_step(): down_part = lax.dot_general(h, z_oth, FIRST, preferred_element_type=F32)  21.3 us
    dot_general x1, matrix products, local_step(): up_part = lax.dot_general(xs, dc_oth, FIRST, preferred_element_type=F32)  19.9 us
  transfers between devices with their start and end apart: 4, of which 2 were waited for; matrix products, arithmetic and copies ran while one was open for 10% of the time, Pallas kernels for 0%

profile of v4, /device:TPU:0, one launch (start us, length us, event | category | flops | bytes accessed | tf_op | source)
XLA Modules:
  0.0 617.8 jit_solution(2197369223250921694)
XLA Ops:
  0.6 426.6 %hidden.1 = (bf16[2048,5120]{1,0:T(8,128)(2,1)}, bf16[2048,2560]{1,0:T(8,128)(2,1)}, bf16[2048,2560]{1,0:T(8,128)(2,1)}, bf16[2048,1280]{1,0:T(8,128)(2,1)}, bf1...) custom-call(bf16[1024,1280]{1,0:T(8,128)(2,1)} %x_in.1, ...), custom_call_target="tpu_custom_call" | custom-call | flops 134217728000 | bytes 200000000 | tf_op jit(solution)/shard_map/hidden/pallas_call | solution.py:280
  427.2 0.0 copy-start.3
  427.3 21.3 %fusion.3 = f32[5120,640]{1,0:T(8,128)S(1)} fusion(bf16[2048,5120]{1,0:T(8,128)(2,1)} %get-tuple-element.24, bf16[2048,640]{1,0:T(8,128)(2,1)} %get-tuple-element.26), kind=kOutput, calls=%fused_computation.6 | convolution fusion | flops 13421772800 | bytes 36700160 | tf_op jit(solution)/shard_map/dot_general | solution.py:313
  448.5 0.9 collective-permute-start.3
  449.4 0.0 copy-done.3
  449.4 0.0 copy-start.1
  449.4 0.0 copy-start
  449.4 19.9 %fusion.2 = f32[1280,2560]{1,0:T(8,128)} fusion(bf16[2048,1280]{1,0:T(8,128)(2,1)S(1)} %copy-done.3, bf16[2048,2560]{1,0:T(8,128)(2,1)} %get-tuple-element.23), kind=kOutput, calls=%fused_computation.5 | convolution fusion | flops 13421772800 | bytes 28835840 | tf_op jit(solution)/shard_map/dot_general | solution.py:314
  469.3 0.0 collective-permute-start.2
  469.4 0.0 copy-done.1
  469.4 1.3 collective-permute-start.1
  470.7 0.0 copy-done
  470.7 0.7 collective-permute-start
  471.4 46.5 %collective-permute-done.1 = bf16[1024,1024]{1,0:T(8,128)(2,1)S(1)} collective-permute-done((bf16[1024,1024]{1,0:T(8,128)(2,1)S(1)}, bf16[1024,1024]{1,0:T(8,128)(2,1)S(1)}, u32[]{:S(2)}, u32[]{:S(2)}) %collective-permute-start.1) | collective-permute-done | bytes 2097184 | tf_op jit(solution)/shard_map/ppermute | solution.py:311
  517.9 0.0 copy-start.2
  517.9 6.5 %fusion.1 = f32[1024,1280]{1,0:T(8,128)} fusion(bf16[1024,1024]{1,0:T(8,128)(2,1)S(1)} %collective-permute-done.1, bf16[1280,1024]{1,0:T(8,128)(2,1)} %get-tuple-element.18), kind=kOutput, calls=%fused_computation.4 | convolution fusion | flops 2684354560 | bytes 9961472 | tf_op jit(solution)/shard_map/dot_general | solution.py:319
  524.4 37.9 %collective-permute-done = bf16[1024,1024]{1,0:T(8,128)(2,1)S(1)} collective-permute-done((bf16[1024,1024]{1,0:T(8,128)(2,1)S(1)}, bf16[1024,1024]{1,0:T(8,128)(2,1)S(1)}, u32[]{:S(2)}, u32[]{:S(2)}) %collective-permute-start) | collective-permute-done | bytes 2097184 | tf_op jit(solution)/shard_map/ppermute | solution.py:312
  562.3 0.0 copy-done.2
  562.3 8.0 %add_convert_fusion.1 = bf16[1024,1280]{1,0:T(8,128)(2,1)} fusion(f32[1024,1280]{1,0:T(8,128)} %fusion.1, f32[1024,1280]{1,0:T(8,128)S(1)} %copy-done.2, f32[1024,1280]{1,0:T(8,128)} %get-tuple-element.20, bf16[1024,1024]{1,0:T(8,128)(2,1)S(1)} %collective-permute-done, bf16[1280,1024]{1,0:T(8,128)(2,1)} %get-tuple-element.16), kind=kOutput, calls=%fused_computation.3 | convolution fusion | flops 2689597440 | bytes 23068672 | tf_op jit(solution)/shard_map/dot_general | solution.py:320
  570.3 0.0 collective-permute-done.3
  570.3 25.5 %add_convert_fusion = bf16[5120,640]{1,0:T(8,128)(2,1)} fusion(f32[5120,640]{1,0:T(8,128)} %collective-permute-done.3, bf16[2048,5120]{1,0:T(8,128)(2,1)} %get-tuple-element.24, bf16[2048,640]{1,0:T(8,128)(2,1)} %get-tuple-element.25), kind=kOutput, calls=%fused_computation.1 | convolution fusion | flops 13428326400 | bytes 43253760 | tf_op jit(solution)/shard_map/dot_general | solution.py:317
  595.8 0.0 collective-permute-done.2
  595.8 22.0 %fusion = bf16[1280,2560]{1,0:T(8,128)(2,1)} fusion(f32[1280,2560]{1,0:T(8,128)} %collective-permute-done.2, bf16[2048,1280]{1,0:T(8,128)(2,1)} %get-tuple-element.21, bf16[2048,2560]{1,0:T(8,128)(2,1)} %get-tuple-element.22), kind=kOutput, calls=%fused_computation.2 | convolution fusion | flops 13428326400 | bytes 35389440 | tf_op jit(solution)/shard_map/dot_general | solution.py:318
Async XLA Ops:
  427.2 22.1 %copy-start.3 = (bf16[2048,1280]{1,0:T(8,128)(2,1)S(1)}, bf16[2048,1280]{1,0:T(8,128)(2,1)}, u32[]{:S(2)}) copy-start(bf16[2048,1280]{1,0:T(8,128)(2,1)} %get-tuple-element.21) | copy-start | bytes 15728644
  448.5 121.7 %collective-permute-start.3 = (f32[5120,640]{1,0:T(8,128)S(1)}, f32[5120,640]{1,0:T(8,128)}, u32[]{:S(2)}, u32[]{:S(2)}) collective-permute-start(f32[5120,640]{1,0:T(8,128)S(1)} %fusion.3), channel_id=1, source_target_pairs={{0,1},{1,0},{2,3},{3,2},{4,5},{5,4},{6,7},{7,6}} | collective-permute-start | bytes 39321608 | tf_op jit(solution)/shard_map/ppermute | solution.py:315
  449.4 20.0 %copy-start.1 = (bf16[1024,1024]{1,0:T(8,128)(2,1)S(1)}, bf16[1024,1024]{1,0:T(8,128)(2,1)}, u32[]{:S(2)}) copy-start(bf16[1024,1024]{1,0:T(8,128)(2,1)} %get-tuple-element.17) | copy-start | bytes 6291460
  449.4 21.3 %copy-start = (bf16[1024,1024]{1,0:T(8,128)(2,1)S(1)}, bf16[1024,1024]{1,0:T(8,128)(2,1)}, u32[]{:S(2)}) copy-start(bf16[1024,1024]{1,0:T(8,128)(2,1)} %get-tuple-element.15) | copy-start | bytes 6291460
  469.3 126.5 %collective-permute-start.2 = (f32[1280,2560]{1,0:T(8,128)}, f32[1280,2560]{1,0:T(8,128)}, u32[]{:S(2)}, u32[]{:S(2)}) collective-permute-start(f32[1280,2560]{1,0:T(8,128)} %fusion.2), channel_id=1, source_target_pairs={{0,1},{1,0},{2,3},{3,2},{4,5},{5,4},{6,7},{7,6}} | collective-permute-start | bytes 39321608 | tf_op jit(solution)/shard_map/ppermute | solution.py:316
  469.4 48.5 %collective-permute-start.1 = (bf16[1024,1024]{1,0:T(8,128)(2,1)S(1)}, bf16[1024,1024]{1,0:T(8,128)(2,1)S(1)}, u32[]{:S(2)}, u32[]{:S(2)}) collective-permute-start(bf16[1024,1024]{1,0:T(8,128)(2,1)S(1)} %copy-done.1), channel_id=1, source_target_pairs={{0,4},{4,0},{1,5},{5,1},{2,6},{6,2},{3,7},{7,3}} | collective-permute-start | bytes 6291464 | tf_op jit(solution)/shard_map/ppermute | solution.py:311
  470.7 91.6 %collective-permute-start = (bf16[1024,1024]{1,0:T(8,128)(2,1)S(1)}, bf16[1024,1024]{1,0:T(8,128)(2,1)S(1)}, u32[]{:S(2)}, u32[]{:S(2)}) collective-permute-start(bf16[1024,1024]{1,0:T(8,128)(2,1)S(1)} %copy-done), channel_id=1, source_target_pairs={{0,4},{4,0},{1,5},{5,1},{2,6},{6,2},{3,7},{7,3}} | collective-permute-start | bytes 6291464 | tf_op jit(solution)/shard_map/ppermute | solution.py:312
  517.9 44.4 %copy-start.2 = (f32[1024,1280]{1,0:T(8,128)S(1)}, f32[1024,1280]{1,0:T(8,128)}, u32[]{:S(2)}) copy-start(f32[1024,1280]{1,0:T(8,128)} %get-tuple-element.19) | copy-start | bytes 15728644

commit v5 on v4

--- a/solution.py
+++ b/solution.py
@@ -31,10 +31,10 @@
 
 
 def hidden_kernel(x_in, up, down, z_in,
-                  h_out, dc_own, dc_oth, x_out, z_own, z_oth, dx_own, dx_part, dx_got, dcp_own, dcp_oth, up_y, up_yd, up_d, up_x, up_xd, down_d, down_x, down_xd,
+                  h_out, dc_out, x_out, z_out, dx_own, dx_part, dx_got, dcp_own, dcp_oth, up_y, up_yd, up_d, up_x, up_xd, down_d, down_x, down_xd,
                   xv, zv, uv, vv, acc, h_st, dc_st,
                   act_send, act_recv, wx_send, wx_recv, wd_send, wd_recv, all_send, all_recv,
-                  load_sem, local_sem, out_sem, extra_sem):
+                  load_sem, local_sem, out_sem, extra_sem, push_send, push_recv):
     cz, cy, cx = lax.axis_index("cz"), lax.axis_index("cy"), lax.axis_index("cx")
     to_x, to_y, to_d = {"cy": 1 - cy}, {"cz": 1 - cz}, {"cx": 1 - cx}
     rows, dk = x_in.shape
@@ -134,17 +134,23 @@
     z0.wait()
     up_all.wait_recv()
     down_all.wait_recv()
-    x_save = pltpu.make_async_copy(xv.at[:, near], x_out, local_sem.at[0])
-    z_save = [pltpu.make_async_copy(zv.at[:, lanes(0, cx)], z_own, local_sem.at[1]),
-              pltpu.make_async_copy(zv.at[:, lanes(0, 1 - cx)], z_oth, local_sem.at[2])]
+    mine_all, core_all = pl.ds(0, 2 * rows), pl.ds(2 * rows, 2 * rows)
+    saves = [pltpu.make_async_copy(xv.at[:, near], x_out.at[mine_all], local_sem.at[0]),
+             pltpu.make_async_copy(zv.at[:, lanes(0, cx)], z_out.at[mine_all], local_sem.at[1])]
+    shares = [remote(xv.at[:, near], x_out.at[core_all], all_send.at[5], all_recv.at[5], to_d),
+              remote(zv.at[:, lanes(0, 1 - cx)], z_out.at[core_all], all_send.at[6], all_recv.at[6], to_d)]
 
     def outs(n, c, r0):
         sl = lax.rem(n, 2)
         r = pl.ds(r0, RB)
         left, right = pl.ds(0, W), pl.ds(W, W)
+        far_r = pl.ds(2 * rows + r0, RB)
         moves = ((h_st.at[sl, :, left], h_out.at[r, frow(cx, c)]), (h_st.at[sl, :, right], h_out.at[r, frow(1 - cx, c)]),
-                 (dc_st.at[sl, :, left], dc_own.at[r, mine(c)]), (dc_st.at[sl, :, right], dc_oth.at[r, mine(c)]))
-        return [pltpu.make_async_copy(src, dst, out_sem.at[sl, i]) for i, (src, dst) in enumerate(moves)]
+                 (dc_st.at[sl, :, left], dc_out.at[r, mine(c)]))
+        pushes = ((h_st.at[sl, :, left], h_out.at[far_r, frow(cx, c)]), (h_st.at[sl, :, right], h_out.at[far_r, frow(1 - cx, c)]),
+                  (dc_st.at[sl, :, right], dc_out.at[far_r, mine(c)]))
+        return ([pltpu.make_async_copy(src, dst, out_sem.at[sl, i]) for i, (src, dst) in enumerate(moves)],
+                [remote(src, dst, push_send.at[sl, i], push_recv.at[n, i], to_d) for i, (src, dst) in enumerate(pushes)])
 
     def extra(n, c):
         sl = lax.rem(n, 2)
@@ -153,6 +159,12 @@
                 pltpu.make_async_copy(dc_st.at[sl, :, pl.ds(W, W)], dcp_oth.at[:, cols], extra_sem.at[1])]
 
     steps = 2 * chunks
+
+    def drain(first, last):
+        @pl.loop(first, last)
+        def _(c):
+            for copy in over_x(c) + over_d(c):
+                copy.wait_send()
 
     @pl.loop(0, steps)
     def _(s):
@@ -187,10 +199,13 @@
 
         @pl.when((s < SLOTS) | (late & ~odd))
         def _():
-            for copy in over_d(c):
-                copy.wait_recv()
-            for copy in loads(c, True):
-                copy.start()
+            @pl.when(s < SLOTS)
+            def _():
+                for copy in over_d(c):
+                    copy.wait_recv()
+                for copy in loads(c, True):
+                    copy.start()
+
             for copy in loads(c, False) + loads(c, True):
                 copy.wait()
 
@@ -198,11 +213,22 @@
         def _():
             x2.wait_recv()
             z2.wait_recv()
-            x_save.start()
-            for copy in z_save:
+            for copy in saves + shares:
                 copy.start()
             x3.wait_recv()
             z3.wait_recv()
+
+        @pl.when(s == steps - 4)
+        def _():
+            for copy in saves:
+                copy.wait()
+            for copy in shares:
+                copy.wait_send()
+                copy.wait_recv()
+            up_tail_d.wait_recv()
+            for copy in (x1, z1, x2, z2, x3, z3, up_all, down_all, up_tail, up_tail_d):
+                copy.wait_send()
+            drain(0, chunks - 4)
 
         @pl.when(s == steps - 1)
         def _():
@@ -218,8 +244,12 @@
 
         @pl.when(s >= 2)
         def _():
-            for copy in outs(s, c, r0):
+            keep, push = outs(s - 2, c, r0)
+            for copy in keep:
                 copy.wait()
+            for copy in push:
+                copy.wait_send()
+                copy.wait_recv()
 
         @pl.when((s >= 2 * split + 3) & odd)
         def _():
@@ -228,36 +258,40 @@
 
         h_st[sl] = h.astype(BF16)
         dc_st[sl] = dc
-        for copy in outs(s, c, r0):
+
+        @pl.when((s >= 2 * SLOTS - 1) & odd & (s < steps - 1))
+        def _():
+            for copy in over_d(hc):
+                copy.wait_recv()
+            for copy in loads(hc, True):
+                copy.start()
+
+        @pl.when((half == 0) | (c < split))
+        def _():
+            acc[pl.ds(r0, RB), :] += lax.dot_general(dc_st[sl], uv[slot, near, :], LAST, preferred_element_type=F32)
+
+        keep, push = outs(s, c, r0)
+        for copy in keep + push:
             copy.start()
 
-        @pl.when((half == 0) | (c < split))
-        def _():
-            acc[pl.ds(r0, RB), :] += lax.dot_general(dc_st[sl], uv[slot, near, :], LAST, preferred_element_type=F32)
-
         @pl.when((half == 1) & (c >= split))
         def _():
             for copy in extra(s, c):
                 copy.start()
 
     for n in range(2):
-        for copy in outs(n, 0, 0):
+        keep, push = outs(steps - 2 + n, 0, 0)
+        for copy in keep:
             copy.wait()
+        for copy in push:
+            copy.wait_send()
+            copy.wait_recv()
     for copy in extra(1, split):
         copy.wait()
     own_save.wait()
-    up_tail_d.wait_recv()
     part_send.wait_recv()
-    x_save.wait()
-    for copy in z_save:
-        copy.wait()
-    for copy in (x1, z1, x2, z2, x3, z3, up_all, down_all, up_tail, up_tail_d, part_send):
-        copy.wait_send()
-
-    @pl.loop(0, chunks)
-    def _(c):
-        for copy in over_x(c) + over_d(c):
-            copy.wait_send()
+    part_send.wait_send()
+    drain(chunks - 4, chunks)
 
 
 def hidden_call(x_act, w_up, w_down, z_grad):
@@ -269,8 +303,7 @@
     hbm = pl.BlockSpec(memory_space=pl.ANY)
     sds = jax.ShapeDtypeStruct
     out_shape = [
-        sds((2 * rows, ff), BF16), sds((2 * rows, ffc), BF16), sds((2 * rows, ffc), BF16),
-        sds((2 * rows, dk), BF16), sds((2 * rows, dq), BF16), sds((2 * rows, dq), BF16),
+        sds((4 * rows, ff), BF16), sds((4 * rows, ffc), BF16), sds((4 * rows, dk), BF16), sds((4 * rows, dq), BF16),
         sds((rows, dk), F32), sds((rows, dk), F32), sds((rows, dk), F32),
         sds((rows, PHI * W), BF16), sds((rows, PHI * W), BF16), sds((dk, PHI * W), BF16), sds((dk, PHI * W), BF16),
         sds(w_up.shape, BF16), sds(w_up.shape, BF16), sds(w_up.shape, BF16),
@@ -288,7 +321,7 @@
             pltpu.VMEM((2 * rows, dk), F32),
             pltpu.VMEM((2, RB, 2 * W), BF16), pltpu.VMEM((2, RB, 2 * W), BF16),
             dma((6,)), dma((6,)), dma((chunks, 3)), dma((chunks, 3)), dma((chunks, 3)), dma((chunks, 3)),
-            dma((5,)), dma((5,)), dma((12,)), dma((5,)), dma((2, 4)), dma((2,)),
+            dma((7,)), dma((7,)), dma((12,)), dma((5,)), dma((2, 3)), dma((2,)), dma((2, 3)), dma((4 * ffc // (2 * W), 3)),
         ],
         compiler_params=pltpu.CompilerParams(
             collective_id=0, has_side_effects=True, vmem_limit_bytes=67_000_000),
@@ -306,16 +339,11 @@
     swap = [(0, 1), (1, 0)]
 
     def local_step(x_act, w_up, w_down, z_grad):
-        (h, dc_own, dc_oth, xs, z_own, z_oth, dx_own, _, dx_got, dcp_own, dcp_oth, up_y, up_yd) = hidden_call(
-            x_act, w_up, w_down, z_grad)[:13]
+        h, dc, xs, zs, dx_own, _, dx_got, dcp_own, dcp_oth, up_y, up_yd = hidden_call(x_act, w_up, w_down, z_grad)[:11]
         dcr_own = lax.ppermute(dcp_own, "cz", swap)
         dcr_oth = lax.ppermute(dcp_oth, "cz", swap)
-        down_part = lax.dot_general(h, z_oth, FIRST, preferred_element_type=F32)
-        up_part = lax.dot_general(xs, dc_oth, FIRST, preferred_element_type=F32)
-        down_got = lax.ppermute(down_part, "cx", swap)
-        up_got = lax.ppermute(up_part, "cx", swap)
-        down_grad = (lax.dot_general(h, z_own, FIRST, preferred_element_type=F32) + down_got).astype(BF16)
-        up_grad = (lax.dot_general(xs, dc_own, FIRST, preferred_element_type=F32) + up_got).astype(BF16)
+        down_grad = lax.dot_general(h, zs, FIRST, preferred_element_type=F32).astype(BF16)
+        up_grad = lax.dot_general(xs, dc, FIRST, preferred_element_type=F32).astype(BF16)
         dx = lax.dot_general(dcr_own, up_y, LAST, preferred_element_type=F32) + (dx_own + dx_got)
         x_grad = (lax.dot_general(dcr_oth, up_yd, LAST, preferred_element_type=F32) + dx).astype(BF16)
         return (x_grad, up_grad, down_grad)

time: 619 us -> 530 us (0.86)
  waiting for transfers between devices: 84.4 us -> 15.2 us
  matrix products: 103 us -> 82.3 us
    ppermute x1, waiting for transfers between devices: 37.9 us -> 0.01 us  [local_step(): dcr_oth = lax.ppermute(dcp_oth, 'cz', swap)]
    ppermute x1, waiting for transfers between devices: 46.5 us -> 15.2 us  [local_step(): dcr_own = lax.ppermute(dcp_own, 'cz', swap)]
    dot_general x4 -> x2, matrix products: 88.7 us -> 75.1 us  [the longest x1 40.2 us: local_step(): lax.dot_general(h, zs, FIRST, preferred_element_type=F32).astype(BF16)]
  transfers between devices with their start and end apart: 4 -> 2, of which waited for: 2 -> 1; matrix products, arithmetic and copies ran while one was open for 10% -> 15% of each run, Pallas kernels for 0% -> 0%
where the time goes in v5:
time: 530 us; the launch traced here: 529 us
  Pallas kernels  429 us (81%)
  matrix products  82.3 us (16%)
  waiting for transfers between devices  15.2 us (3%)
    pallas_call x1, Pallas kernels, hidden_call(): pl.pallas_call(hidden_kernel, in_specs=[hbm] * 4, out_specs=[hbm] * len(o...  429 us
    dot_general x1, matrix products, local_step(): lax.dot_general(h, zs, FIRST, preferred_element_type=F32).astype(BF16)  40.2 us
    dot_general x1, matrix products, local_step(): lax.dot_general(xs, dc, FIRST, preferred_element_type=F32).astype(BF16)  34.8 us
    ppermute x1, waiting for transfers between devices, local_step(): dcr_own = lax.ppermute(dcp_own, 'cz', swap)  15.2 us
  transfers between devices with their start and end apart: 2, of which 1 were waited for; matrix products, arithmetic and copies ran while one was open for 15% of the time, Pallas kernels for 0%

profile of v5, /device:TPU:0, one launch (start us, length us, event | category | flops | bytes accessed | tf_op | source)
XLA Modules:
  0.0 529.1 jit_solution(11424522331960449939)
XLA Ops:
  0.6 428.8 %hidden.1 = (bf16[4096,5120]{1,0:T(8,128)(2,1)}, bf16[4096,2560]{1,0:T(8,128)(2,1)}, bf16[4096,1280]{1,0:T(8,128)(2,1)}, bf16[4096,640]{1,0:T(8,128)(2,1)}, f32[...) custom-call(bf16[1024,1280]{1,0:T(8,128)(2,1)} %x_in.1, ...), custom_call_target="tpu_custom_call" | custom-call | flops 134217728000 | bytes 200000000 | tf_op jit(solution)/shard_map/hidden/pallas_call | solution.py:313
  429.4 1.6 collective-permute-start
  431.0 0.5 collective-permute-start.1
  431.5 0.0 slice-start
  431.5 0.0 slice-start.2
  431.5 40.2 %convolution_convert_fusion.1 = bf16[5120,640]{1,0:T(8,128)(2,1)} fusion(bf16[4096,5120]{1,0:T(8,128)(2,1)} %get-tuple-element.21, bf16[4096,640]{1,0:T(8,128)(2,1)} %get-tuple-element.22), kind=kOutput, calls=%fused_computation.1 | convolution fusion | flops 26846822400 | bytes 53739520 | tf_op jit(solution)/shard_map/dot_general | solution.py:345
  471.7 0.0 copy-start.1
  471.7 0.0 slice-start.1
  471.7 0.0 slice-start.3
  471.7 34.8 %convolution_convert_fusion = bf16[1280,2560]{1,0:T(8,128)(2,1)} fusion(bf16[4096,1280]{1,0:T(8,128)(2,1)} %get-tuple-element.19, bf16[4096,2560]{1,0:T(8,128)(2,1)} %get-tuple-element.20), kind=kOutput, calls=%fused_computation | convolution fusion | flops 26846822400 | bytes 38010880 | tf_op jit(solution)/shard_map/dot_general | solution.py:346
  506.6 15.2 %collective-permute-done.1 = bf16[1024,1024]{1,0:T(8,128)(2,1)S(1)} collective-permute-done((bf16[1024,1024]{1,0:T(8,128)(2,1)}, bf16[1024,1024]{1,0:T(8,128)(2,1)S(1)}, u32[]{:S(2)}, u32[]{:S(2)}) %collective-permute-start.1) | collective-permute-done | bytes 2097184 | tf_op jit(solution)/shard_map/ppermute | solution.py:343
  521.7 0.0 copy-done.1
  521.7 0.0 copy-start
  521.7 2.9 fusion
  524.6 0.0 collective-permute-done
  524.7 0.0 slice-done
  524.7 0.0 slice-done.2
  524.7 0.0 slice-done.1
  524.7 0.0 slice-done.3
  524.7 0.0 copy-done
  524.7 4.3 add_convert_fusion
  (2 shorter events, 0.0 us)
Async XLA Ops:
  429.4 95.2 %collective-permute-start = (bf16[1024,1024]{1,0:T(8,128)(2,1)}, bf16[1024,1024]{1,0:T(8,128)(2,1)S(1)}, u32[]{:S(2)}, u32[]{:S(2)}) collective-permute-start(bf16[1024,1024]{1,0:T(8,128)(2,1)} %get-tuple-element.13), channel_id=1, source_target_pairs={{0,4},{4,0},{1,5},{5,1},{2,6},{6,2},{3,7},{7,3}} | collective-permute-start | bytes 6291464 | tf_op jit(solution)/shard_map/ppermute | solution.py:344
  431.0 90.7 %collective-permute-start.1 = (bf16[1024,1024]{1,0:T(8,128)(2,1)}, bf16[1024,1024]{1,0:T(8,128)(2,1)S(1)}, u32[]{:S(2)}, u32[]{:S(2)}) collective-permute-start(bf16[1024,1024]{1,0:T(8,128)(2,1)} %get-tuple-element.15), channel_id=1, source_target_pairs={{0,4},{4,0},{1,5},{5,1},{2,6},{6,2},{3,7},{7,3}} | collective-permute-start | bytes 6291464 | tf_op jit(solution)/shard_map/ppermute | solution.py:343
  431.5 93.2 %slice-start = ((s8[5242880]{0:T(1024)(128)(4,1)}), s8[4194304]{0:T(1024)(128)(4,1)S(1)}, s32[]{:S(2)}) async-start(s8[5242880]{0:T(1024)(128)(4,1)} %bitcast.8), calls=%async_computation | async-start | bytes 8388608
  431.5 93.2 %slice-start.2 = ((s8[5242880]{0:T(1024)(128)(4,1)}), s8[4194304]{0:T(1024)(128)(4,1)S(1)}, s32[]{:S(2)}) async-start(s8[5242880]{0:T(1024)(128)(4,1)} %bitcast.10), calls=%async_computation.2 | async-start | bytes 8388608
  471.7 50.0 %copy-start.1 = (bf16[1280,1024]{1,0:T(8,128)(2,1)S(1)}, bf16[1280,1024]{1,0:T(8,128)(2,1)}, u32[]{:S(2)}) copy-start(bf16[1280,1024]{1,0:T(8,128)(2,1)} %get-tuple-element.16) | copy-start | bytes 7864324
  471.7 53.0 %slice-start.1 = ((s8[5242880]{0:T(1024)(128)(4,1)}), s8[1048576]{0:T(1024)(128)(4,1)S(1)}, s32[]{:S(2)}) async-start(s8[5242880]{0:T(1024)(128)(4,1)} %bitcast.8), calls=%async_computation.1 | async-start | bytes 2097152
  471.7 53.0 %slice-start.3 = ((s8[5242880]{0:T(1024)(128)(4,1)}), s8[1048576]{0:T(1024)(128)(4,1)S(1)}, s32[]{:S(2)}) async-start(s8[5242880]{0:T(1024)(128)(4,1)} %bitcast.10), calls=%async_computation.3 | async-start | bytes 2097152
  521.7 3.0 copy-start

commit v6 on v5

--- a/solution.py
+++ b/solution.py
@@ -168,13 +168,45 @@
 
     @pl.loop(0, steps)
     def _(s):
-        late = s >= 2 * SLOTS
-        c = jnp.where(late, SLOTS + (s - 2 * SLOTS) // 2, lax.rem(s, SLOTS))
-        half = jnp.where(late, jnp.where(c < split, 1 - lax.rem(s, 2), lax.rem(s, 2)), s // SLOTS)
+        paired = s >= 2 * split
+        c = jnp.where(paired, s // 2, jnp.where(s < SLOTS, s, jnp.where(s < SLOTS + split, s - SLOTS, s - split)))
+        half = jnp.where(paired, lax.rem(s, 2), jnp.where((s >= SLOTS) & (s < SLOTS + split), 1, 0))
         odd = lax.rem(s, 2) == 1
-        hc = jnp.where(s < SLOTS, s, SLOTS + (s - 2 * SLOTS + 1) // 2)
-
-        @pl.when(s == 2 * split - 1)
+        single = (s >= 2 * SLOTS - 1) & (s < SLOTS + split - 1)
+        ahead = single | ((s >= 2 * split - 1) & odd & (s < steps - 1))
+        hc = jnp.where(single, s - SLOTS + 1, (s + 1) // 2)
+
+        def arrive(c):
+            for copy in over_x(c):
+                copy.wait_recv()
+            for copy in over_d(c):
+                copy.start()
+
+            @pl.when(c + AHEAD < chunks)
+            def _():
+                for copy in over_x(c + AHEAD):
+                    copy.start()
+
+            for copy in loads(c, False):
+                copy.start()
+
+        def arrive_late(c):
+            for copy in over_d(c):
+                copy.wait_recv()
+            for copy in loads(c, True):
+                copy.start()
+
+        @pl.when(s < SLOTS)
+        def _():
+            arrive(s)
+            arrive_late(s)
+
+        @pl.when((s < SLOTS) | ((s >= 2 * SLOTS) & (s < SLOTS + split)) | (paired & ~odd))
+        def _():
+            for copy in loads(c, False) + loads(c, True):
+                copy.wait()
+
+        @pl.when(s == SLOTS + split)
         def _():
             part_save.start()
             up_tail.wait_recv()
@@ -182,32 +214,9 @@
             part_save.wait()
             part_send.start()
 
-        @pl.when((s < SLOTS) | ((s >= 2 * SLOTS - 1) & odd & (s < steps - 1)))
-        def _():
-            for copy in over_x(hc):
-                copy.wait_recv()
-            for copy in over_d(hc):
-                copy.start()
-
-            @pl.when(hc + AHEAD < chunks)
-            def _():
-                for copy in over_x(hc + AHEAD):
-                    copy.start()
-
-            for copy in loads(hc, False):
-                copy.start()
-
-        @pl.when((s < SLOTS) | (late & ~odd))
-        def _():
-            @pl.when(s < SLOTS)
-            def _():
-                for copy in over_d(c):
-                    copy.wait_recv()
-                for copy in loads(c, True):
-                    copy.start()
-
-            for copy in loads(c, False) + loads(c, True):
-                copy.wait()
+        @pl.when(ahead)
+        def _():
+            arrive(hc)
 
         @pl.when(s == SLOTS)
         def _():
@@ -259,12 +268,9 @@
         h_st[sl] = h.astype(BF16)
         dc_st[sl] = dc
 
-        @pl.when((s >= 2 * SLOTS - 1) & odd & (s < steps - 1))
-        def _():
-            for copy in over_d(hc):
-                copy.wait_recv()
-            for copy in loads(hc, True):
-                copy.start()
+        @pl.when(ahead)
+        def _():
+            arrive_late(hc)
 
         @pl.when((half == 0) | (c < split))
         def _():

time: 530 us -> 519 us (0.979)
  Pallas kernels: 429 us -> 418 us
    pallas_call x1, Pallas kernels: 429 us -> 418 us  [hidden_call(): pl.pallas_call(hidden_kernel, in_specs=[hbm] * 4, out_specs=[hbm] * len(o...]
where the time goes in v6:
time: 519 us
  Pallas kernels  418 us (81%)
  matrix products  82.3 us (16%)
  waiting for transfers between devices  16 us (3%)
    pallas_call x1, Pallas kernels, hidden_call(): pl.pallas_call(hidden_kernel, in_specs=[hbm] * 4, out_specs=[hbm] * len(o...  418 us
    dot_general x1, matrix products, local_step(): lax.dot_general(h, zs, FIRST, preferred_element_type=F32).astype(BF16)  40.2 us
    dot_general x1, matrix products, local_step(): lax.dot_general(xs, dc, FIRST, preferred_element_type=F32).astype(BF16)  34.8 us
    ppermute x1, waiting for transfers between devices, local_step(): dcr_own = lax.ppermute(dcp_own, 'cz', swap)  16 us
  transfers between devices with their start and end apart: 2, of which 1 were waited for; matrix products, arithmetic and copies ran while one was open for 15% of the time, Pallas kernels for 0%

profile of v6, /device:TPU:0, one launch (start us, length us, event | category | flops | bytes accessed | tf_op | source)
XLA Modules:
  0.0 518.6 jit_solution(1900348462576891518)
XLA Ops:
  0.6 417.5 %hidden.1 = (bf16[4096,5120]{1,0:T(8,128)(2,1)}, bf16[4096,2560]{1,0:T(8,128)(2,1)}, bf16[4096,1280]{1,0:T(8,128)(2,1)}, bf16[4096,640]{1,0:T(8,128)(2,1)}, f32[...) custom-call(bf16[1024,1280]{1,0:T(8,128)(2,1)} %x_in.1, ...), custom_call_target="tpu_custom_call" | custom-call | flops 134217728000 | bytes 200000000 | tf_op jit(solution)/shard_map/hidden/pallas_call | solution.py:319
  418.2 1.0 collective-permute-start
  419.1 1.1 collective-permute-start.1
  420.2 0.0 slice-start
  420.2 0.0 slice-start.2
  420.2 40.2 %convolution_convert_fusion.1 = bf16[5120,640]{1,0:T(8,128)(2,1)} fusion(bf16[4096,5120]{1,0:T(8,128)(2,1)} %get-tuple-element.21, bf16[4096,640]{1,0:T(8,128)(2,1)} %get-tuple-element.22), kind=kOutput, calls=%fused_computation.1 | convolution fusion | flops 26846822400 | bytes 53739520 | tf_op jit(solution)/shard_map/dot_general | solution.py:351
  460.4 0.0 copy-start.1
  460.4 0.0 slice-start.1
  460.4 0.0 slice-start.3
  460.4 34.8 %convolution_convert_fusion = bf16[1280,2560]{1,0:T(8,128)(2,1)} fusion(bf16[4096,1280]{1,0:T(8,128)(2,1)} %get-tuple-element.19, bf16[4096,2560]{1,0:T(8,128)(2,1)} %get-tuple-element.20), kind=kOutput, calls=%fused_computation | convolution fusion | flops 26846822400 | bytes 38010880 | tf_op jit(solution)/shard_map/dot_general | solution.py:352
  495.3 16.0 %collective-permute-done.1 = bf16[1024,1024]{1,0:T(8,128)(2,1)S(1)} collective-permute-done((bf16[1024,1024]{1,0:T(8,128)(2,1)}, bf16[1024,1024]{1,0:T(8,128)(2,1)S(1)}, u32[]{:S(2)}, u32[]{:S(2)}) %collective-permute-start.1) | collective-permute-done | bytes 2097184 | tf_op jit(solution)/shard_map/ppermute | solution.py:349
  511.2 0.0 copy-done.1
  511.3 0.0 copy-start
  511.3 2.9 fusion
  514.2 0.0 collective-permute-done
  514.2 0.0 slice-done
  514.2 0.0 slice-done.2
  514.2 0.0 slice-done.1
  514.2 0.0 slice-done.3
  514.2 0.0 copy-done
  514.3 4.3 add_convert_fusion
  (2 shorter events, 0.0 us)
Async XLA Ops:
  418.2 96.0 %collective-permute-start = (bf16[1024,1024]{1,0:T(8,128)(2,1)}, bf16[1024,1024]{1,0:T(8,128)(2,1)S(1)}, u32[]{:S(2)}, u32[]{:S(2)}) collective-permute-start(bf16[1024,1024]{1,0:T(8,128)(2,1)} %get-tuple-element.13), channel_id=1, source_target_pairs={{0,4},{4,0},{1,5},{5,1},{2,6},{6,2},{3,7},{7,3}} | collective-permute-start | bytes 6291464 | tf_op jit(solution)/shard_map/ppermute | solution.py:350
  419.1 92.1 %collective-permute-start.1 = (bf16[1024,1024]{1,0:T(8,128)(2,1)}, bf16[1024,1024]{1,0:T(8,128)(2,1)S(1)}, u32[]{:S(2)}, u32[]{:S(2)}) collective-permute-start(bf16[1024,1024]{1,0:T(8,128)(2,1)} %get-tuple-element.15), channel_id=1, source_target_pairs={{0,4},{4,0},{1,5},{5,1},{2,6},{6,2},{3,7},{7,3}} | collective-permute-start | bytes 6291464 | tf_op jit(solution)/shard_map/ppermute | solution.py:349
  420.2 94.0 %slice-start = ((s8[5242880]{0:T(1024)(128)(4,1)}), s8[4194304]{0:T(1024)(128)(4,1)S(1)}, s32[]{:S(2)}) async-start(s8[5242880]{0:T(1024)(128)(4,1)} %bitcast.8), calls=%async_computation | async-start | bytes 8388608
  420.2 94.0 %slice-start.2 = ((s8[5242880]{0:T(1024)(128)(4,1)}), s8[4194304]{0:T(1024)(128)(4,1)S(1)}, s32[]{:S(2)}) async-start(s8[5242880]{0:T(1024)(128)(4,1)} %bitcast.10), calls=%async_computation.2 | async-start | bytes 8388608
  460.4 50.8 %copy-start.1 = (bf16[1280,1024]{1,0:T(8,128)(2,1)S(1)}, bf16[1280,1024]{1,0:T(8,128)(2,1)}, u32[]{:S(2)}) copy-start(bf16[1280,1024]{1,0:T(8,128)(2,1)} %get-tuple-element.16) | copy-start | bytes 7864324
  460.4 53.8 %slice-start.1 = ((s8[5242880]{0:T(1024)(128)(4,1)}), s8[1048576]{0:T(1024)(128)(4,1)S(1)}, s32[]{:S(2)}) async-start(s8[5242880]{0:T(1024)(128)(4,1)} %bitcast.8), calls=%async_computation.1 | async-start | bytes 2097152
  460.4 53.8 %slice-start.3 = ((s8[5242880]{0:T(1024)(128)(4,1)}), s8[1048576]{0:T(1024)(128)(4,1)S(1)}, s32[]{:S(2)}) async-start(s8[5242880]{0:T(1024)(128)(4,1)} %bitcast.10), calls=%async_computation.3 | async-start | bytes 2097152
  511.3 3.0 copy-start

commit v7 on v6

--- a/solution.py
+++ b/solution.py
@@ -31,7 +31,7 @@
 
 
 def hidden_kernel(x_in, up, down, z_in,
-                  h_out, dc_out, x_out, z_out, dx_own, dx_part, dx_got, dcp_own, dcp_oth, up_y, up_yd, up_d, up_x, up_xd, down_d, down_x, down_xd,
+                  h_out, dc_out, x_out, z_out, dx_own, dx_part, dx_got, dc_first, dc_got, dcp_own, dcp_oth, up_y0, up_y, up_yd, up_d, up_x, up_xd, down_d, down_x, down_xd,
                   xv, zv, uv, vv, acc, h_st, dc_st,
                   act_send, act_recv, wx_send, wx_recv, wd_send, wd_recv, all_send, all_recv,
                   load_sem, local_sem, out_sem, extra_sem, push_send, push_recv):
@@ -65,9 +65,12 @@
     down_all = remote(down, down_d, all_send.at[1], all_recv.at[1], to_d)
 
     split = chunks - PHI
-    tail = pl.ds(split * W, PHI * W)
-    up_tail = remote(up.at[:, tail], up_y, all_send.at[2], all_recv.at[2], to_y)
-    up_tail_d = remote(up_y, up_yd, all_send.at[3], all_recv.at[3], to_d)
+    head, tail = pl.ds(split * W, W), pl.ds((split + 1) * W, (PHI - 1) * W)
+    up_tail = [remote(up.at[:, head], up_y0, all_send.at[2], all_recv.at[2], to_y),
+               remote(up.at[:, tail], up_y, all_send.at[7], all_recv.at[7], to_y)]
+    up_tail_d = [remote(up_y0, up_yd.at[:, pl.ds(0, W)], all_send.at[3], all_recv.at[3], to_d),
+                 remote(up_y, up_yd.at[:, pl.ds(W, (PHI - 1) * W)], all_send.at[8], all_recv.at[8], to_d)]
+    first_send = remote(dc_first, dc_got, all_send.at[9], all_recv.at[9], to_y)
     part_save = pltpu.make_async_copy(acc.at[oth], dx_part, local_sem.at[3])
     part_send = remote(dx_part, dx_got, all_send.at[4], all_recv.at[4], to_y)
     own_save = pltpu.make_async_copy(acc.at[own], dx_own, local_sem.at[4])
@@ -129,7 +132,8 @@
     x3.start()
     z1.wait_recv()
     z3.start()
-    up_tail.start()
+    for copy in up_tail:
+        copy.start()
     x0.wait()
     z0.wait()
     up_all.wait_recv()
@@ -152,11 +156,12 @@
         return ([pltpu.make_async_copy(src, dst, out_sem.at[sl, i]) for i, (src, dst) in enumerate(moves)],
                 [remote(src, dst, push_send.at[sl, i], push_recv.at[n, i], to_d) for i, (src, dst) in enumerate(pushes)])
 
-    def extra(n, c):
+    def extra(n, c, first):
         sl = lax.rem(n, 2)
-        cols = pl.ds(pl.multiple_of((c - split) * W, W), W)
-        return [pltpu.make_async_copy(dc_st.at[sl, :, pl.ds(0, W)], dcp_own.at[:, cols], extra_sem.at[0]),
-                pltpu.make_async_copy(dc_st.at[sl, :, pl.ds(W, W)], dcp_oth.at[:, cols], extra_sem.at[1])]
+        base = pl.ds(pl.multiple_of((c - split) * W, W), W)
+        own_dst = dc_first if first else dcp_own.at[:, pl.ds(pl.multiple_of((c - split - 1) * W, W), W)]
+        return [pltpu.make_async_copy(dc_st.at[sl, :, pl.ds(0, W)], own_dst, extra_sem.at[0]),
+                pltpu.make_async_copy(dc_st.at[sl, :, pl.ds(W, W)], dcp_oth.at[:, base], extra_sem.at[1])]
 
     steps = 2 * chunks
 
@@ -209,8 +214,9 @@
         @pl.when(s == SLOTS + split)
         def _():
             part_save.start()
-            up_tail.wait_recv()
-            up_tail_d.start()
+            for copy, onward in zip(up_tail, up_tail_d):
+                copy.wait_recv()
+                onward.start()
             part_save.wait()
             part_send.start()
 
@@ -234,8 +240,9 @@
             for copy in shares:
                 copy.wait_send()
                 copy.wait_recv()
-            up_tail_d.wait_recv()
-            for copy in (x1, z1, x2, z2, x3, z3, up_all, down_all, up_tail, up_tail_d):
+            for copy in up_tail_d:
+                copy.wait_recv()
+            for copy in [x1, z1, x2, z2, x3, z3, up_all, down_all] + up_tail + up_tail_d:
                 copy.wait_send()
             drain(0, chunks - 4)
 
@@ -262,8 +269,12 @@
 
         @pl.when((s >= 2 * split + 3) & odd)
         def _():
-            for copy in extra(s, c):
+            for copy in extra(s, c, True):
                 copy.wait()
+
+        @pl.when(s == 2 * split + 3)
+        def _():
+            first_send.start()
 
         h_st[sl] = h.astype(BF16)
         dc_st[sl] = dc
@@ -280,9 +291,14 @@
         for copy in keep + push:
             copy.start()
 
-        @pl.when((half == 1) & (c >= split))
-        def _():
-            for copy in extra(s, c):
+        @pl.when((half == 1) & (c == split))
+        def _():
+            for copy in extra(s, c, True):
+                copy.start()
+
+        @pl.when((half == 1) & (c > split))
+        def _():
+            for copy in extra(s, c, False):
                 copy.start()
 
     for n in range(2):
@@ -292,11 +308,13 @@
         for copy in push:
             copy.wait_send()
             copy.wait_recv()
-    for copy in extra(1, split):
+    for copy in extra(1, split, True):
         copy.wait()
     own_save.wait()
     part_send.wait_recv()
     part_send.wait_send()
+    first_send.wait_recv()
+    first_send.wait_send()
     drain(chunks - 4, chunks)
 
 
@@ -311,7 +329,8 @@
     out_shape = [
         sds((4 * rows, ff), BF16), sds((4 * rows, ffc), BF16), sds((4 * rows, dk), BF16), sds((4 * rows, dq), BF16),
         sds((rows, dk), F32), sds((rows, dk), F32), sds((rows, dk), F32),
-        sds((rows, PHI * W), BF16), sds((rows, PHI * W), BF16), sds((dk, PHI * W), BF16), sds((dk, PHI * W), BF16),
+        sds((rows, W), BF16), sds((rows, W), BF16), sds((rows, (PHI - 1) * W), BF16), sds((rows, PHI * W), BF16),
+        sds((dk, W), BF16), sds((dk, (PHI - 1) * W), BF16), sds((dk, PHI * W), BF16),
         sds(w_up.shape, BF16), sds(w_up.shape, BF16), sds(w_up.shape, BF16),
         sds(w_down.shape, BF16), sds(w_down.shape, BF16), sds(w_down.shape, BF16),
     ]
@@ -327,7 +346,7 @@
             pltpu.VMEM((2 * rows, dk), F32),
             pltpu.VMEM((2, RB, 2 * W), BF16), pltpu.VMEM((2, RB, 2 * W), BF16),
             dma((6,)), dma((6,)), dma((chunks, 3)), dma((chunks, 3)), dma((chunks, 3)), dma((chunks, 3)),
-            dma((7,)), dma((7,)), dma((12,)), dma((5,)), dma((2, 3)), dma((2,)), dma((2, 3)), dma((4 * ffc // (2 * W), 3)),
+            dma((10,)), dma((10,)), dma((12,)), dma((5,)), dma((2, 3)), dma((2,)), dma((2, 3)), dma((4 * ffc // (2 * W), 3)),
         ],
         compiler_params=pltpu.CompilerParams(
             collective_id=0, has_side_effects=True, vmem_limit_bytes=67_000_000),
@@ -345,12 +364,14 @@
     swap = [(0, 1), (1, 0)]
 
     def local_step(x_act, w_up, w_down, z_grad):
-        h, dc, xs, zs, dx_own, _, dx_got, dcp_own, dcp_oth, up_y, up_yd = hidden_call(x_act, w_up, w_down, z_grad)[:11]
+        (h, dc, xs, zs, dx_own, _, dx_got, _, dc_got, dcp_own, dcp_oth, up_y0, up_y, up_yd) = hidden_call(
+            x_act, w_up, w_down, z_grad)[:14]
         dcr_own = lax.ppermute(dcp_own, "cz", swap)
         dcr_oth = lax.ppermute(dcp_oth, "cz", swap)
         down_grad = lax.dot_general(h, zs, FIRST, preferred_element_type=F32).astype(BF16)
         up_grad = lax.dot_general(xs, dc, FIRST, preferred_element_type=F32).astype(BF16)
-        dx = lax.dot_general(dcr_own, up_y, LAST, preferred_element_type=F32) + (dx_own + dx_got)
+        dx = lax.dot_general(dc_got, up_y0, LAST, preferred_element_type=F32) + (dx_own + dx_got)
+        dx = lax.dot_general(dcr_own, up_y, LAST, preferred_element_type=F32) + dx
         x_grad = (lax.dot_general(dcr_oth, up_yd, LAST, preferred_element_type=F32) + dx).astype(BF16)
         return (x_grad, up_grad, down_grad)
 

time: 519 us -> 516 us (level)
  waiting for transfers between devices: 16 us -> 2.33 us
  matrix products: 82.3 us -> 87.7 us
    ppermute x1, waiting for transfers between devices: 16 us -> 0.01 us  [local_step(): dcr_own = lax.ppermute(dcp_own, 'cz', swap)]
  transfers between devices with their start and end apart: 2 -> 2, of which waited for: 1 -> 1; matrix products, arithmetic and copies ran while one was open for 15% -> 16% of each run, Pallas kernels for 0% -> 0%
where the time goes in v7:
time: 516 us; the launch traced here: 515 us
  Pallas kernels  421 us (82%)
  matrix products  87.7 us (17%)
    pallas_call x1, Pallas kernels, hidden_call(): pl.pallas_call(hidden_kernel, in_specs=[hbm] * 4, out_specs=[hbm] * len(o...  421 us
    dot_general x1, matrix products, local_step(): lax.dot_general(h, zs, FIRST, preferred_element_type=F32).astype(BF16)  40.2 us
    dot_general x1, matrix products, local_step(): lax.dot_general(xs, dc, FIRST, preferred_element_type=F32).astype(BF16)  34.7 us
  transfers between devices with their start and end apart: 2, of which 1 were waited for; matrix products, arithmetic and copies ran while one was open for 16% of the time, Pallas kernels for 0%

profile of v7, /device:TPU:0, one launch (start us, length us, event | category | flops | bytes accessed | tf_op | source)
XLA Modules:
  0.0 515.0 jit_solution(6027625593804934388)
XLA Ops:
  0.6 421.5 %hidden.1 = (bf16[4096,5120]{1,0:T(8,128)(2,1)}, bf16[4096,2560]{1,0:T(8,128)(2,1)}, bf16[4096,1280]{1,0:T(8,128)(2,1)}, bf16[4096,640]{1,0:T(8,128)(2,1)}, f32[...) custom-call(bf16[1024,1280]{1,0:T(8,128)(2,1)} %x_in.1, ...), custom_call_target="tpu_custom_call" | custom-call | flops 134217728000 | bytes 200000000 | tf_op jit(solution)/shard_map/hidden/pallas_call | solution.py:338
  422.1 1.5 collective-permute-start.1
  423.6 0.5 collective-permute-start
  424.2 40.2 %convolution_convert_fusion.1 = bf16[5120,640]{1,0:T(8,128)(2,1)} fusion(bf16[4096,5120]{1,0:T(8,128)(2,1)} %get-tuple-element.25, bf16[4096,640]{1,0:T(8,128)(2,1)} %get-tuple-element.26), kind=kOutput, calls=%fused_computation.1 | convolution fusion | flops 26846822400 | bytes 53739520 | tf_op jit(solution)/shard_map/dot_general | solution.py:371
  464.3 0.0 copy-start
  464.3 0.0 copy-start.1
  464.3 34.7 %convolution_convert_fusion = bf16[1280,2560]{1,0:T(8,128)(2,1)} fusion(bf16[4096,1280]{1,0:T(8,128)(2,1)} %get-tuple-element.23, bf16[4096,2560]{1,0:T(8,128)(2,1)} %get-tuple-element.24), kind=kOutput, calls=%fused_computation | convolution fusion | flops 26846822400 | bytes 38010880 | tf_op jit(solution)/shard_map/dot_general | solution.py:372
  499.0 0.0 copy-start.2
  499.0 0.0 copy-done
  499.0 0.0 copy-done.1
  499.0 0.0 slice-start
  499.1 0.0 slice-start.2
  499.1 0.8 fusion.1
  499.9 0.0 collective-permute-done.1
  499.9 0.8 copy-done.2
  500.7 0.0 slice-start.1
  500.7 0.0 slice-start.3
  500.7 4.6 fusion
  505.3 2.3 collective-permute-done
  507.6 0.0 slice-done
  507.6 0.0 slice-done.2
  507.6 0.0 slice-done.1
  507.6 0.0 slice-done.3
  507.7 7.3 %add_convert_fusion = bf16[1024,1280]{1,0:T(8,128)(2,1)} fusion(f32[1024,1280]{1,0:T(8,128)} %fusion, f32[1024,1280]{1,0:T(8,128)S(1)} %fusion.1, f32[1024,1280]{1,0:T(8,128)S(1)} %bitcast.11, f32[1024,1280]{1,0:T(8,128)S(1)} %bitcast.13, bf16[1024,1024]{1,0:T(8,128)(2,1)S(1)} %collective-permute-done, bf16[1280,1024]{1,0:T(8,128)(2,1)} %get-tuple-element.16), kind=kOutput, calls=%fused_computation.2 | convolution fusion | flops 2690908160 | bytes 28311552 | tf_op jit(solution)/shard_map/dot_general | solution.py:375
  (2 shorter events, 0.0 us)
Async XLA Ops:
  422.1 77.8 %collective-permute-start.1 = (bf16[1024,896]{1,0:T(8,128)(2,1)}, bf16[1024,896]{1,0:T(8,128)(2,1)S(1)}, u32[]{:S(2)}, u32[]{:S(2)}) collective-permute-start(bf16[1024,896]{1,0:T(8,128)(2,1)} %get-tuple-element.17), channel_id=1, source_target_pairs={{0,4},{4,0},{1,5},{5,1},{2,6},{6,2},{3,7},{7,3}} | collective-permute-start | bytes 5505032 | tf_op jit(solution)/shard_map/ppermute | solution.py:369
  423.6 84.0 %collective-permute-start = (bf16[1024,1024]{1,0:T(8,128)(2,1)}, bf16[1024,1024]{1,0:T(8,128)(2,1)S(1)}, u32[]{:S(2)}, u32[]{:S(2)}) collective-permute-start(bf16[1024,1024]{1,0:T(8,128)(2,1)} %get-tuple-element.15), channel_id=1, source_target_pairs={{0,4},{4,0},{1,5},{5,1},{2,6},{6,2},{3,7},{7,3}} | collective-permute-start | bytes 6291464 | tf_op jit(solution)/shard_map/ppermute | solution.py:370
  464.3 34.7 %copy-start = (bf16[1280,128]{1,0:T(8,128)(2,1)S(1)}, bf16[1280,128]{1,0:T(8,128)(2,1)}, u32[]{:S(2)}) copy-start(bf16[1280,128]{1,0:T(8,128)(2,1)} %get-tuple-element.20) | copy-start | bytes 983044
  464.3 34.7 %copy-start.1 = (bf16[1024,128]{1,0:T(8,128)(2,1)S(1)}, bf16[1024,128]{1,0:T(8,128)(2,1)}, u32[]{:S(2)}) copy-start(bf16[1024,128]{1,0:T(8,128)(2,1)} %get-tuple-element.19) | copy-start | bytes 786436
  499.0 1.6 copy-start.2
  499.0 8.6 %slice-start = ((s8[5242880]{0:T(1024)(128)(4,1)}), s8[4194304]{0:T(1024)(128)(4,1)S(1)}, s32[]{:S(2)}) async-start(s8[5242880]{0:T(1024)(128)(4,1)} %bitcast.10), calls=%async_computation | async-start | bytes 8388608
  499.1 8.6 %slice-start.2 = ((s8[5242880]{0:T(1024)(128)(4,1)}), s8[4194304]{0:T(1024)(128)(4,1)S(1)}, s32[]{:S(2)}) async-start(s8[5242880]{0:T(1024)(128)(4,1)} %bitcast.12), calls=%async_computation.2 | async-start | bytes 8388608
  500.7 7.0 %slice-start.1 = ((s8[5242880]{0:T(1024)(128)(4,1)}), s8[1048576]{0:T(1024)(128)(4,1)S(1)}, s32[]{:S(2)}) async-start(s8[5242880]{0:T(1024)(128)(4,1)} %bitcast.10), calls=%async_computation.1 | async-start | bytes 2097152
  500.7 7.0 %slice-start.3 = ((s8[5242880]{0:T(1024)(128)(4,1)}), s8[1048576]{0:T(1024)(128)(4,1)S(1)}, s32[]{:S(2)}) async-start(s8[5242880]{0:T(1024)(128)(4,1)} %bitcast.12), calls=%async_computation.3 | async-start | bytes 2097152

commit v8 on v7

--- a/solution.py
+++ b/solution.py
@@ -253,10 +253,6 @@
         slot = lax.rem(c, SLOTS)
         r0 = pl.multiple_of(half * rows, RB)
         sl = lax.rem(s, 2)
-        cc = jnp.dot(xv[pl.ds(r0, RB), :], uv[slot], preferred_element_type=F32)
-        dh = lax.dot_general(zv[pl.ds(r0, RB), :], vv[slot], LAST, preferred_element_type=F32)
-        h, slope = gelu_parts(cc.astype(BF16).astype(F32))
-        dc = (dh * slope).astype(BF16)
 
         @pl.when(s >= 2)
         def _():
@@ -276,8 +272,16 @@
         def _():
             first_send.start()
 
-        h_st[sl] = h.astype(BF16)
-        dc_st[sl] = dc
+        part = RB // 2
+        pre = []
+        for q in range(2):
+            cc = jnp.dot(xv[pl.ds(r0 + q * part, part), :], uv[slot], preferred_element_type=F32)
+            dh = lax.dot_general(zv[pl.ds(r0 + q * part, part), :], vv[slot], LAST, preferred_element_type=F32)
+            pre.append((cc, dh))
+        for q, (cc, dh) in enumerate(pre):
+            h, slope = gelu_parts(cc.astype(BF16).astype(F32))
+            h_st[sl, pl.ds(q * part, part), :] = h.astype(BF16)
+            dc_st[sl, pl.ds(q * part, part), :] = (dh * slope).astype(BF16)
 
         @pl.when(ahead)
         def _():
@@ -371,7 +375,9 @@
         down_grad = lax.dot_general(h, zs, FIRST, preferred_element_type=F32).astype(BF16)
         up_grad = lax.dot_general(xs, dc, FIRST, preferred_element_type=F32).astype(BF16)
         dx = lax.dot_general(dc_got, up_y0, LAST, preferred_element_type=F32) + (dx_own + dx_got)
+        dx = lax.optimization_barrier(dx)
         dx = lax.dot_general(dcr_own, up_y, LAST, preferred_element_type=F32) + dx
+        dx = lax.optimization_barrier(dx)
         x_grad = (lax.dot_general(dcr_oth, up_yd, LAST, preferred_element_type=F32) + dx).astype(BF16)
         return (x_grad, up_grad, down_grad)
 

time: 516 us -> 515 us (level)
  matrix products: 87.7 us -> 80 us
  waiting for transfers between devices: 2.33 us -> 7.95 us
    ppermute x1, waiting for transfers between devices: 2.33 us -> 7.95 us  [local_step(): dcr_oth = lax.ppermute(dcp_oth, 'cz', swap)]
  transfers between devices with their start and end apart: 2 -> 2, of which waited for: 1 -> 1; matrix products, arithmetic and copies ran while one was open for 16% -> 15% of each run, Pallas kernels for 0% -> 0%
where the time goes in v8:
time: 515 us
  Pallas kernels  423 us (82%)
  matrix products  80 us (16%)
  waiting for transfers between devices  7.95 us (2%)
    pallas_call x1, Pallas kernels, hidden_call(): pl.pallas_call(hidden_kernel, in_specs=[hbm] * 4, out_specs=[hbm] * len(o...  423 us
    dot_general x1, matrix products, local_step(): lax.dot_general(h, zs, FIRST, preferred_element_type=F32).astype(BF16)  40.2 us
    dot_general x1, matrix products, local_step(): lax.dot_general(xs, dc, FIRST, preferred_element_type=F32).astype(BF16)  31.8 us
  transfers between devices with their start and end apart: 2, of which 1 were waited for; matrix products, arithmetic and copies ran while one was open for 15% of the time, Pallas kernels for 0%

profile of v8, /device:TPU:0, one launch (start us, length us, event | category | flops | bytes accessed | tf_op | source)
XLA Modules:
  0.0 514.5 jit_solution(2890172277730282648)
XLA Ops:
  0.6 423.0 %hidden.1 = (bf16[4096,5120]{1,0:T(8,128)(2,1)}, bf16[4096,2560]{1,0:T(8,128)(2,1)}, bf16[4096,1280]{1,0:T(8,128)(2,1)}, bf16[4096,640]{1,0:T(8,128)(2,1)}, f32[...) custom-call(bf16[1024,1280]{1,0:T(8,128)(2,1)} %x_in.1, ...), custom_call_target="tpu_custom_call" | custom-call | flops 134217728000 | bytes 200000000 | tf_op jit(solution)/shard_map/hidden/pallas_call | solution.py:342
  423.7 1.5 collective-permute-start.1
  425.2 0.5 collective-permute-start
  425.7 0.0 copy-start.4
  425.7 0.0 slice-start
  425.7 0.0 slice-start.2
  425.7 40.2 %convolution_convert_fusion.1 = bf16[5120,640]{1,0:T(8,128)(2,1)} fusion(bf16[4096,5120]{1,0:T(8,128)(2,1)} %get-tuple-element.25, bf16[4096,640]{1,0:T(8,128)(2,1)} %get-tuple-element.26), kind=kOutput, calls=%fused_computation.1 | convolution fusion | flops 26846822400 | bytes 53739520 | tf_op jit(solution)/shard_map/dot_general | solution.py:375
  465.9 0.0 copy-done.4
  465.9 0.0 slice-start.1
  465.9 0.0 slice-start.3
  466.0 0.0 copy-start
  466.0 0.0 copy-start.1
  466.0 31.8 %convolution_convert_fusion = bf16[1280,2560]{1,0:T(8,128)(2,1)} fusion(bf16[4096,1280]{1,0:T(8,128)(2,1)S(1)} %copy-done.4, bf16[4096,2560]{1,0:T(8,128)(2,1)} %get-tuple-element.24), kind=kOutput, calls=%fused_computation | convolution fusion | flops 26846822400 | bytes 38010880 | tf_op jit(solution)/shard_map/dot_general | solution.py:376
  497.7 0.0 slice-done
  497.7 0.0 slice-done.2
  497.7 0.0 slice-done.1
  497.7 0.0 slice-done.3
  497.8 0.0 copy-done
  497.8 0.0 copy-done.1
  497.8 0.0 copy-start.2
  497.8 0.9 add_add_fusion
  498.7 0.0 collective-permute-done.1
  498.7 0.8 copy-done.2
  499.4 0.0 copy-start.3
  499.4 2.9 convolution_add_fusion
  502.4 7.9 %collective-permute-done = bf16[1024,1024]{1,0:T(8,128)(2,1)S(1)} collective-permute-done((bf16[1024,1024]{1,0:T(8,128)(2,1)}, bf16[1024,1024]{1,0:T(8,128)(2,1)S(1)}, u32[]{:S(2)}, u32[]{:S(2)}) %collective-permute-start) | collective-permute-done | bytes 2097184 | tf_op jit(solution)/shard_map/ppermute | solution.py:374
  510.3 0.0 copy-done.3
  510.3 4.2 add_convert_fusion
  (2 shorter events, 0.0 us)
Async XLA Ops:
  423.7 75.0 %collective-permute-start.1 = (bf16[1024,896]{1,0:T(8,128)(2,1)}, bf16[1024,896]{1,0:T(8,128)(2,1)S(1)}, u32[]{:S(2)}, u32[]{:S(2)}) collective-permute-start(bf16[1024,896]{1,0:T(8,128)(2,1)} %get-tuple-element.17), channel_id=1, source_target_pairs={{0,4},{4,0},{1,5},{5,1},{2,6},{6,2},{3,7},{7,3}} | collective-permute-start | bytes 5505032 | tf_op jit(solution)/shard_map/ppermute | solution.py:373
  425.2 85.1 %collective-permute-start = (bf16[1024,1024]{1,0:T(8,128)(2,1)}, bf16[1024,1024]{1,0:T(8,128)(2,1)S(1)}, u32[]{:S(2)}, u32[]{:S(2)}) collective-permute-start(bf16[1024,1024]{1,0:T(8,128)(2,1)} %get-tuple-element.15), channel_id=1, source_target_pairs={{0,4},{4,0},{1,5},{5,1},{2,6},{6,2},{3,7},{7,3}} | collective-permute-start | bytes 6291464 | tf_op jit(solution)/shard_map/ppermute | solution.py:374
  425.7 40.2 %copy-start.4 = (bf16[4096,1280]{1,0:T(8,128)(2,1)S(1)}, bf16[4096,1280]{1,0:T(8,128)(2,1)}, u32[]{:S(2)}) copy-start(bf16[4096,1280]{1,0:T(8,128)(2,1)} %get-tuple-element.23) | copy-start | bytes 31457284
  425.7 72.0 %slice-start = ((s8[5242880]{0:T(1024)(128)(4,1)}), s8[1048576]{0:T(1024)(128)(4,1)S(1)}, s32[]{:S(2)}) async-start(s8[5242880]{0:T(1024)(128)(4,1)} %bitcast.10), calls=%async_computation | async-start | bytes 2097152
  425.7 72.0 %slice-start.2 = ((s8[5242880]{0:T(1024)(128)(4,1)}), s8[4194304]{0:T(1024)(128)(4,1)S(1)}, s32[]{:S(2)}) async-start(s8[5242880]{0:T(1024)(128)(4,1)} %bitcast.12), calls=%async_computation.2 | async-start | bytes 8388608
  465.9 31.8 %slice-start.1 = ((s8[5242880]{0:T(1024)(128)(4,1)}), s8[4194304]{0:T(1024)(128)(4,1)S(1)}, s32[]{:S(2)}) async-start(s8[5242880]{0:T(1024)(128)(4,1)} %bitcast.10), calls=%async_computation.1 | async-start | bytes 8388608
  465.9 31.8 %slice-start.3 = ((s8[5242880]{0:T(1024)(128)(4,1)}), s8[1048576]{0:T(1024)(128)(4,1)S(1)}, s32[]{:S(2)}) async-start(s8[5242880]{0:T(1024)(128)(4,1)} %bitcast.12), calls=%async_computation.3 | async-start | bytes 2097152
  466.0 31.8 %copy-start = (bf16[1280,128]{1,0:T(8,128)(2,1)S(1)}, bf16[1280,128]{1,0:T(8,128)(2,1)}, u32[]{:S(2)}) copy-start(bf16[1280,128]{1,0:T(8,128)(2,1)} %get-tuple-element.20) | copy-start | bytes 983044
  466.0 31.8 %copy-start.1 = (bf16[1024,128]{1,0:T(8,128)(2,1)S(1)}, bf16[1024,128]{1,0:T(8,128)(2,1)}, u32[]{:S(2)}) copy-start(bf16[1024,128]{1,0:T(8,128)(2,1)} %get-tuple-element.19) | copy-start | bytes 786436
  497.8 1.6 copy-start.2
  499.4 10.9 %copy-start.3 = (bf16[1280,1024]{1,0:T(8,128)(2,1)S(1)}, bf16[1280,1024]{1,0:T(8,128)(2,1)}, u32[]{:S(2)}) copy-start(bf16[1280,1024]{1,0:T(8,128)(2,1)} %get-tuple-element.16) | copy-start | bytes 7864324

commit v9 on v8

--- a/solution.py
+++ b/solution.py
@@ -18,6 +18,7 @@
 W = 128
 RB = 1024
 PHI = 8
+END = 3
 AHEAD = 8
 SLOTS = 8
 
@@ -31,7 +32,7 @@
 
 
 def hidden_kernel(x_in, up, down, z_in,
-                  h_out, dc_out, x_out, z_out, dx_own, dx_part, dx_got, dc_first, dc_got, dcp_own, dcp_oth, up_y0, up_y, up_yd, up_d, up_x, up_xd, down_d, down_x, down_xd,
+                  h_out, dc_out, x_out, z_out, dx_own, dx_part, dx_got, dc_first, dc_got, dcp_own, dcp_mid, dcp_end, up_y0, up_y, up_yd, up_ye, up_d, up_x, up_xd, down_d, down_x, down_xd,
                   xv, zv, uv, vv, acc, h_st, dc_st,
                   act_send, act_recv, wx_send, wx_recv, wd_send, wd_recv, all_send, all_recv,
                   load_sem, local_sem, out_sem, extra_sem, push_send, push_recv):
@@ -65,11 +66,14 @@
     down_all = remote(down, down_d, all_send.at[1], all_recv.at[1], to_d)
 
     split = chunks - PHI
+    mid = PHI - END
     head, tail = pl.ds(split * W, W), pl.ds((split + 1) * W, (PHI - 1) * W)
     up_tail = [remote(up.at[:, head], up_y0, all_send.at[2], all_recv.at[2], to_y),
                remote(up.at[:, tail], up_y, all_send.at[7], all_recv.at[7], to_y)]
     up_tail_d = [remote(up_y0, up_yd.at[:, pl.ds(0, W)], all_send.at[3], all_recv.at[3], to_d),
-                 remote(up_y, up_yd.at[:, pl.ds(W, (PHI - 1) * W)], all_send.at[8], all_recv.at[8], to_d)]
+                 remote(up_y.at[:, pl.ds(0, (mid - 1) * W)], up_yd.at[:, pl.ds(W, (mid - 1) * W)],
+                        all_send.at[8], all_recv.at[8], to_d),
+                 remote(up_y.at[:, pl.ds((mid - 1) * W, END * W)], up_ye, all_send.at[10], all_recv.at[10], to_d)]
     first_send = remote(dc_first, dc_got, all_send.at[9], all_recv.at[9], to_y)
     part_save = pltpu.make_async_copy(acc.at[oth], dx_part, local_sem.at[3])
     part_send = remote(dx_part, dx_got, all_send.at[4], all_recv.at[4], to_y)
@@ -156,12 +160,16 @@
         return ([pltpu.make_async_copy(src, dst, out_sem.at[sl, i]) for i, (src, dst) in enumerate(moves)],
                 [remote(src, dst, push_send.at[sl, i], push_recv.at[n, i], to_d) for i, (src, dst) in enumerate(pushes)])
 
-    def extra(n, c, first):
+    def extra(n, c, first, last):
         sl = lax.rem(n, 2)
-        base = pl.ds(pl.multiple_of((c - split) * W, W), W)
-        own_dst = dc_first if first else dcp_own.at[:, pl.ds(pl.multiple_of((c - split - 1) * W, W), W)]
+
+        def block(start):
+            return pl.ds(pl.multiple_of((c - start) * W, W), W)
+
+        own_dst = dc_first if first else dcp_own.at[:, block(split + 1)]
+        oth_dst = dcp_end.at[:, block(split + mid)] if last else dcp_mid.at[:, block(split)]
         return [pltpu.make_async_copy(dc_st.at[sl, :, pl.ds(0, W)], own_dst, extra_sem.at[0]),
-                pltpu.make_async_copy(dc_st.at[sl, :, pl.ds(W, W)], dcp_oth.at[:, base], extra_sem.at[1])]
+                pltpu.make_async_copy(dc_st.at[sl, :, pl.ds(W, W)], oth_dst, extra_sem.at[1])]
 
     steps = 2 * chunks
 
@@ -214,9 +222,10 @@
         @pl.when(s == SLOTS + split)
         def _():
             part_save.start()
-            for copy, onward in zip(up_tail, up_tail_d):
-                copy.wait_recv()
-                onward.start()
+            for copy in up_tail:
+                copy.wait_recv()
+            for copy in up_tail_d:
+                copy.start()
             part_save.wait()
             part_send.start()
 
@@ -265,7 +274,7 @@
 
         @pl.when((s >= 2 * split + 3) & odd)
         def _():
-            for copy in extra(s, c, True):
+            for copy in extra(s, split, True, False):
                 copy.wait()
 
         @pl.when(s == 2 * split + 3)
@@ -297,12 +306,17 @@
 
         @pl.when((half == 1) & (c == split))
         def _():
-            for copy in extra(s, c, True):
-                copy.start()
-
-        @pl.when((half == 1) & (c > split))
-        def _():
-            for copy in extra(s, c, False):
+            for copy in extra(s, c, True, False):
+                copy.start()
+
+        @pl.when((half == 1) & (c > split) & (c < split + mid))
+        def _():
+            for copy in extra(s, c, False, False):
+                copy.start()
+
+        @pl.when((half == 1) & (c >= split + mid))
+        def _():
+            for copy in extra(s, c, False, True):
                 copy.start()
 
     for n in range(2):
@@ -312,7 +326,7 @@
         for copy in push:
             copy.wait_send()
             copy.wait_recv()
-    for copy in extra(1, split, True):
+    for copy in extra(1, split, True, False):
         copy.wait()
     own_save.wait()
     part_send.wait_recv()
@@ -333,8 +347,10 @@
     out_shape = [
         sds((4 * rows, ff), BF16), sds((4 * rows, ffc), BF16), sds((4 * rows, dk), BF16), sds((4 * rows, dq), BF16),
         sds((rows, dk), F32), sds((rows, dk), F32), sds((rows, dk), F32),
-        sds((rows, W), BF16), sds((rows, W), BF16), sds((rows, (PHI - 1) * W), BF16), sds((rows, PHI * W), BF16),
-        sds((dk, W), BF16), sds((dk, (PHI - 1) * W), BF16), sds((dk, PHI * W), BF16),
+        sds((rows, W), BF16), sds((rows, W), BF16), sds((rows, (PHI - 1) * W), BF16),
+        sds((rows, (PHI - END) * W), BF16), sds((rows, END * W), BF16),
+        sds((dk, W), BF16), sds((dk, (PHI - 1) * W), BF16),
+        sds((dk, (PHI - END) * W), BF16), sds((dk, END * W), BF16),
         sds(w_up.shape, BF16), sds(w_up.shape, BF16), sds(w_up.shape, BF16),
         sds(w_down.shape, BF16), sds(w_down.shape, BF16), sds(w_down.shape, BF16),
     ]
@@ -350,7 +366,7 @@
             pltpu.VMEM((2 * rows, dk), F32),
             pltpu.VMEM((2, RB, 2 * W), BF16), pltpu.VMEM((2, RB, 2 * W), BF16),
             dma((6,)), dma((6,)), dma((chunks, 3)), dma((chunks, 3)), dma((chunks, 3)), dma((chunks, 3)),
-            dma((10,)), dma((10,)), dma((12,)), dma((5,)), dma((2, 3)), dma((2,)), dma((2, 3)), dma((4 * ffc // (2 * W), 3)),
+            dma((11,)), dma((11,)), dma((12,)), dma((5,)), dma((2, 3)), dma((2,)), dma((2, 3)), dma((4 * ffc // (2 * W), 3)),
         ],
         compiler_params=pltpu.CompilerParams(
             collective_id=0, has_side_effects=True, vmem_limit_bytes=67_000_000),
@@ -368,17 +384,20 @@
     swap = [(0, 1), (1, 0)]
 
     def local_step(x_act, w_up, w_down, z_grad):
-        (h, dc, xs, zs, dx_own, _, dx_got, _, dc_got, dcp_own, dcp_oth, up_y0, up_y, up_yd) = hidden_call(
-            x_act, w_up, w_down, z_grad)[:14]
+        (h, dc, xs, zs, dx_own, _, dx_got, _, dc_got, dcp_own, dcp_mid, dcp_end, up_y0, up_y, up_yd, up_ye) = hidden_call(
+            x_act, w_up, w_down, z_grad)[:16]
         dcr_own = lax.ppermute(dcp_own, "cz", swap)
-        dcr_oth = lax.ppermute(dcp_oth, "cz", swap)
+        dcr_mid = lax.ppermute(dcp_mid, "cz", swap)
+        dcr_end = lax.ppermute(dcp_end, "cz", swap)
         down_grad = lax.dot_general(h, zs, FIRST, preferred_element_type=F32).astype(BF16)
         up_grad = lax.dot_general(xs, dc, FIRST, preferred_element_type=F32).astype(BF16)
         dx = lax.dot_general(dc_got, up_y0, LAST, preferred_element_type=F32) + (dx_own + dx_got)
         dx = lax.optimization_barrier(dx)
         dx = lax.dot_general(dcr_own, up_y, LAST, preferred_element_type=F32) + dx
         dx = lax.optimization_barrier(dx)
-        x_grad = (lax.dot_general(dcr_oth, up_yd, LAST, preferred_element_type=F32) + dx).astype(BF16)
+        dx = lax.dot_general(dcr_mid, up_yd, LAST, preferred_element_type=F32) + dx
+        dx = lax.optimization_barrier(dx)
+        x_grad = (lax.dot_general(dcr_end, up_ye, LAST, preferred_element_type=F32) + dx).astype(BF16)
         return (x_grad, up_grad, down_grad)
 
     return jax.shard_map(local_step, mesh=mesh, in_specs=(row_spec, up_spec, down_spec, row_spec), out_specs=(row_spec, up_out, down_out), check_vma=False)

time: 515 us -> 519 us (level)
    ppermute x1 -> x2, waiting for transfers between devices: 7.95 us -> 0.01 us  [the longest x1 0.01 us: local_step(): dcr_end = lax.ppermute(dcp_end, 'cz', swap)]
    ppermute x1, waiting for transfers between devices: 0.01 us -> 7.13 us  [local_step(): dcr_own = lax.ppermute(dcp_own, 'cz', swap)]
  transfers between devices with their start and end apart: 2 -> 3, of which waited for: 1 -> 1; matrix products, arithmetic and copies ran while one was open for 15% -> 16% of each run, Pallas kernels for 0% -> 0%
where the time goes in v9:
time: 519 us
  Pallas kernels  423 us (82%)
  matrix products  84.2 us (16%)
  waiting for transfers between devices  7.13 us (1%)
    pallas_call x1, Pallas kernels, hidden_call(): pl.pallas_call(hidden_kernel, in_specs=[hbm] * 4, out_specs=[hbm] * len(o...  423 us
    dot_general x1, matrix products, local_step(): lax.dot_general(h, zs, FIRST, preferred_element_type=F32).astype(BF16)  40.2 us
    dot_general x1, matrix products, local_step(): lax.dot_general(xs, dc, FIRST, preferred_element_type=F32).astype(BF16)  34.8 us
  transfers between devices with their start and end apart: 3, of which 1 were waited for; matrix products, arithmetic and copies ran while one was open for 16% of the time, Pallas kernels for 0%

profile of v9, /device:TPU:0, one launch (start us, length us, event | category | flops | bytes accessed | tf_op | source)
XLA Modules:
  0.0 518.8 jit_solution(13823098428462005003)
XLA Ops:
  0.6 423.1 %hidden.1 = (bf16[4096,5120]{1,0:T(8,128)(2,1)}, bf16[4096,2560]{1,0:T(8,128)(2,1)}, bf16[4096,1280]{1,0:T(8,128)(2,1)}, bf16[4096,640]{1,0:T(8,128)(2,1)}, f32[...) custom-call(bf16[1024,1280]{1,0:T(8,128)(2,1)} %x_in.1, ...), custom_call_target="tpu_custom_call" | custom-call | flops 134217728000 | bytes 200000000 | tf_op jit(solution)/shard_map/hidden/pallas_call | solution.py:358
  423.8 1.5 collective-permute-start
  425.3 0.5 collective-permute-start.1
  425.8 1.5 collective-permute-start.2
  427.3 0.0 slice-start
  427.3 0.0 slice-start.2
  427.3 40.2 %convolution_convert_fusion.1 = bf16[5120,640]{1,0:T(8,128)(2,1)} fusion(bf16[4096,5120]{1,0:T(8,128)(2,1)} %get-tuple-element.29, bf16[4096,640]{1,0:T(8,128)(2,1)} %get-tuple-element.30), kind=kOutput, calls=%fused_computation.1 | convolution fusion | flops 26846822400 | bytes 53739520 | tf_op jit(solution)/shard_map/dot_general | solution.py:392
  467.5 0.0 slice-start.1
  467.5 0.0 slice-start.3
  467.5 0.0 copy-start.2
  467.5 0.0 copy-start.3
  467.5 34.8 %convolution_convert_fusion = bf16[1280,2560]{1,0:T(8,128)(2,1)} fusion(bf16[4096,1280]{1,0:T(8,128)(2,1)} %get-tuple-element.27, bf16[4096,2560]{1,0:T(8,128)(2,1)} %get-tuple-element.28), kind=kOutput, calls=%fused_computation | convolution fusion | flops 26846822400 | bytes 38010880 | tf_op jit(solution)/shard_map/dot_general | solution.py:393
  502.4 0.0 slice-done
  502.4 0.0 slice-done.2
  502.4 0.0 slice-done.1
  502.4 0.0 slice-done.3
  502.4 0.0 copy-done.2
  502.4 0.0 copy-done.3
  502.4 0.0 copy-start.4
  502.4 0.8 add_add_fusion
  503.3 7.1 %collective-permute-done.2 = bf16[1024,896]{1,0:T(8,128)(2,1)S(1)} collective-permute-done((bf16[1024,896]{1,0:T(8,128)(2,1)}, bf16[1024,896]{1,0:T(8,128)(2,1)S(1)}, u32[]{:S(2)}, u32[]{:S(2)}) %collective-permute-start.2) | collective-permute-done | bytes 1835040 | tf_op jit(solution)/shard_map/ppermute | solution.py:389
  510.4 0.0 copy-done.4
  510.4 0.0 copy-start
  510.4 2.9 convolution_add_fusion
  513.3 0.0 collective-permute-done.1
  513.3 0.0 copy-done
  513.4 0.0 copy-start.1
  513.4 2.3 convolution_add_fusion.1
  515.7 0.0 collective-permute-done
  515.7 0.0 copy-done.1
  515.7 3.1 add_convert_fusion
  (2 shorter events, 0.0 us)
Async XLA Ops:
  423.8 91.9 %collective-permute-start = (bf16[1024,384]{1,0:T(8,128)(2,1)}, bf16[1024,384]{1,0:T(8,128)(2,1)S(1)}, u32[]{:S(2)}, u32[]{:S(2)}) collective-permute-start(bf16[1024,384]{1,0:T(8,128)(2,1)} %get-tuple-element.17), channel_id=1, source_target_pairs={{0,4},{4,0},{1,5},{5,1},{2,6},{6,2},{3,7},{7,3}} | collective-permute-start | bytes 2359304 | tf_op jit(solution)/shard_map/ppermute | solution.py:391
  425.3 88.1 %collective-permute-start.1 = (bf16[1024,640]{1,0:T(8,128)(2,1)}, bf16[1024,640]{1,0:T(8,128)(2,1)S(1)}, u32[]{:S(2)}, u32[]{:S(2)}) collective-permute-start(bf16[1024,640]{1,0:T(8,128)(2,1)} %get-tuple-element.19), channel_id=1, source_target_pairs={{0,4},{4,0},{1,5},{5,1},{2,6},{6,2},{3,7},{7,3}} | collective-permute-start | bytes 3932168 | tf_op jit(solution)/shard_map/ppermute | solution.py:390
  425.8 84.6 %collective-permute-start.2 = (bf16[1024,896]{1,0:T(8,128)(2,1)}, bf16[1024,896]{1,0:T(8,128)(2,1)S(1)}, u32[]{:S(2)}, u32[]{:S(2)}) collective-permute-start(bf16[1024,896]{1,0:T(8,128)(2,1)} %get-tuple-element.21), channel_id=1, source_target_pairs={{0,4},{4,0},{1,5},{5,1},{2,6},{6,2},{3,7},{7,3}} | collective-permute-start | bytes 5505032 | tf_op jit(solution)/shard_map/ppermute | solution.py:389
  427.3 75.1 %slice-start = ((s8[5242880]{0:T(1024)(128)(4,1)}), s8[1048576]{0:T(1024)(128)(4,1)S(1)}, s32[]{:S(2)}) async-start(s8[5242880]{0:T(1024)(128)(4,1)} %bitcast.12), calls=%async_computation | async-start | bytes 2097152
  427.3 75.1 %slice-start.2 = ((s8[5242880]{0:T(1024)(128)(4,1)}), s8[4194304]{0:T(1024)(128)(4,1)S(1)}, s32[]{:S(2)}) async-start(s8[5242880]{0:T(1024)(128)(4,1)} %bitcast.14), calls=%async_computation.2 | async-start | bytes 8388608
  467.5 34.9 %slice-start.1 = ((s8[5242880]{0:T(1024)(128)(4,1)}), s8[4194304]{0:T(1024)(128)(4,1)S(1)}, s32[]{:S(2)}) async-start(s8[5242880]{0:T(1024)(128)(4,1)} %bitcast.12), calls=%async_computation.1 | async-start | bytes 8388608
  467.5 34.9 %slice-start.3 = ((s8[5242880]{0:T(1024)(128)(4,1)}), s8[1048576]{0:T(1024)(128)(4,1)S(1)}, s32[]{:S(2)}) async-start(s8[5242880]{0:T(1024)(128)(4,1)} %bitcast.14), calls=%async_computation.3 | async-start | bytes 2097152
  467.5 34.9 %copy-start.2 = (bf16[1280,128]{1,0:T(8,128)(2,1)S(1)}, bf16[1280,128]{1,0:T(8,128)(2,1)}, u32[]{:S(2)}) copy-start(bf16[1280,128]{1,0:T(8,128)(2,1)} %get-tuple-element.24) | copy-start | bytes 983044
  467.5 34.9 %copy-start.3 = (bf16[1024,128]{1,0:T(8,128)(2,1)S(1)}, bf16[1024,128]{1,0:T(8,128)(2,1)}, u32[]{:S(2)}) copy-start(bf16[1024,128]{1,0:T(8,128)(2,1)} %get-tuple-element.23) | copy-start | bytes 786436
  502.4 8.0 %copy-start.4 = (bf16[1280,896]{1,0:T(8,128)(2,1)S(1)}, bf16[1280,896]{1,0:T(8,128)(2,1)}, u32[]{:S(2)}) copy-start(bf16[1280,896]{1,0:T(8,128)(2,1)} %get-tuple-element.22) | copy-start | bytes 6881284
  510.4 2.9 copy-start
  513.4 2.3 copy-start.1
